TPU v7x, 32 devices: a whole 2x2x4 slice. The times are simulated.
32 devices in a mesh: seq: 8 (over y, x, core), batch: 4 (over z).
Axes of the slice: x: 2, y: 2, z: 4, core: 2. Of those that a mesh axis runs over, the one named last changes fastest.
Arguments:
- inputs: bfloat16 [4, 1024, 1024], P('batch', 'seq'), may hold values from -6 to 6
- lengths: int32 [4], P('batch'), may hold values from 256 to 1024, as said below
- w_qkv: bfloat16 [1024, 3072], P(('seq', 'batch')), may hold values from -0.1875 to 0.1875
- w_out: bfloat16 [1024, 1024], P(('seq', 'batch')), may hold values from -0.1875 to 0.1875
- w_up: bfloat16 [1024, 4096], P(('seq', 'batch')), may hold values from -0.1875 to 0.1875
- w_down: bfloat16 [4096, 1024], P(('seq', 'batch')), may hold values from -0.09375 to 0.09375
- norm_gains: bfloat16 [3, 1024], P(None, ('seq', 'batch')), may hold values from 0.5 to 1.5
- model_biases: bfloat16 [5, 1024], P(None, ('seq', 'batch')), may hold values from -4 to 4
- attn_biases: bfloat16 [2, 1024], P(None, ('seq', 'batch')), may hold values from -0.3125 to 0.3125
- ff_gain: bfloat16 [4096], P(('seq', 'batch')), may hold values from 0.5 to 1.5
- ff_biases: bfloat16 [2, 4096], P(None, ('seq', 'batch')), may hold values from -4 to 4
- head_scale: bfloat16 [16], replicated, may hold values from 0.5 to 2
- cotangent: bfloat16 [4, 1024, 1024], P('batch', 'seq'), may hold values from -6 to 6
Outputs:
- output: bfloat16 [4, 1024, 1024], P('batch', 'seq')
- grad_input: bfloat16 [4, 1024, 1024], P('batch', 'seq')
- grad_qkv: float32 [1024, 3072], P(('seq', 'batch'))
- grad_out: float32 [1024, 1024], P(('seq', 'batch'))
- grad_up: float32 [1024, 4096], P(('seq', 'batch'))
- grad_down: float32 [4096, 1024], P(('seq', 'batch'))
- grad_norm_gains: float32 [3, 1024], P(None, ('seq', 'batch'))
- grad_model_biases: float32 [5, 1024], P(None, ('seq', 'batch'))
- grad_attn_biases: float32 [2, 1024], P(None, ('seq', 'batch'))
- grad_ff_gain: float32 [4096], P(('seq', 'batch'))
- grad_ff_biases: float32 [2, 4096], P(None, ('seq', 'batch'))
- grad_head_scale: float32 [16], replicated
Inputs may be any that keep to these rules, and one draw needn't show every extreme that they name: `lengths`: the number of leading valid rows of each sequence; every draw has one sequence with 1024 valid rows and one with 256.
All inputs are finite; a program needn't handle non-finite values.
Results may differ from a plain program's by a relative error of at most 0.01.
Values may be sent and summed in bfloat16 or wider, within the bound.
A program may use at most 192 MiB of HBM per device.

v0:
```python
import jax
import jax.numpy as jnp
from jax import lax
from jax.sharding import PartitionSpec as P

H = 16
HD = 64


NORM_EPSILON = 1e-05


def layer_norm(vector, norm_gain, norm_bias):
    centered = vector - jnp.mean(vector, axis=-1, keepdims=True)
    spread = jnp.mean(centered * centered, axis=-1, keepdims=True)
    return centered * lax.rsqrt(spread + NORM_EPSILON) * norm_gain + norm_bias


def gelu_norm(hidden, norm_gain, norm_bias):
    return layer_norm(jax.nn.gelu(hidden, approximate=False), norm_gain, norm_bias)


def contract_rows(left, right):
    return lax.dot_general(
        left, right, (((0,), (0,)), ((), ())), preferred_element_type=jnp.float32
    )


def times_transposed(left, right):
    return lax.dot_general(
        left, right, (((1,), (1,)), ((), ())), preferred_element_type=jnp.float32
    )


def shards(
    inputs,
    lengths,
    w_qkv,
    w_out,
    w_up,
    w_down,
    norm_gains,
    model_biases,
    attn_biases,
    ff_gain,
    ff_biases,
    head_scale,
    cotangent,
):
    gathered = (
        lax.all_gather(w_qkv, ("seq", "batch"), axis=0, tiled=True),
        lax.all_gather(w_out, ("seq", "batch"), axis=0, tiled=True),
        lax.all_gather(w_up, ("seq", "batch"), axis=0, tiled=True),
        lax.all_gather(w_down, ("seq", "batch"), axis=0, tiled=True),
        lax.all_gather(norm_gains, ("seq", "batch"), axis=1, tiled=True),
        lax.all_gather(model_biases, ("seq", "batch"), axis=1, tiled=True),
        lax.all_gather(attn_biases, ("seq", "batch"), axis=1, tiled=True),
        lax.all_gather(ff_gain, ("seq", "batch"), axis=0, tiled=True),
        lax.all_gather(ff_biases, ("seq", "batch"), axis=1, tiled=True),
    )
    qkv_full, out_full, up_full, down_full = (gathered[0], gathered[1], gathered[2], gathered[3])
    gain_rows = gathered[4].astype(jnp.float32)
    bias_rows = gathered[5].astype(jnp.float32)
    attn_rows = gathered[6].astype(jnp.float32)
    ffn_gain = gathered[7].astype(jnp.float32)
    ffn_rows = gathered[8].astype(jnp.float32)
    scales = head_scale.astype(jnp.float32)
    local_rows = inputs.shape[1]
    model_width = inputs.shape[2]
    seq_length = local_rows * lax.axis_size("seq")
    tile_rows = min(512, seq_length)
    first_row = lax.axis_index("seq") * local_rows
    valid_rows = lengths[0]
    positions = first_row + jnp.arange(local_rows, dtype=jnp.int32)
    valid_mask = (positions < valid_rows)[:, None]
    score_scale = HD ** (-0.5)
    residual_in = inputs[0].astype(jnp.float32)
    normed, norm_a_pull = jax.vjp(layer_norm, residual_in, gain_rows[0], bias_rows[0])
    normed_low = normed.astype(jnp.bfloat16)
    offsets = jnp.concatenate([bias_rows[3], jnp.zeros_like(bias_rows[3]), attn_rows[0]])
    projected = (
        jnp.dot(normed_low, qkv_full, preferred_element_type=jnp.float32) + offsets
    ).astype(jnp.bfloat16)
    queries = projected[:, :model_width]
    key_local = projected[:, model_width : 2 * model_width]
    value_local = projected[:, 2 * model_width :]
    key_rows, value_rows = (
        lax.all_gather(key_local, "seq", axis=0, tiled=True),
        lax.all_gather(value_local, "seq", axis=0, tiled=True),
    )
    query_heads = queries.reshape(local_rows, H, HD)
    last_needed = jnp.minimum(first_row + local_rows - 1, valid_rows - 1)
    tile_count = last_needed // tile_rows + 1

    def tile_scores(j):
        start = j * tile_rows
        key_tile = lax.dynamic_slice_in_dim(key_rows, start, tile_rows, 0).reshape(tile_rows, H, HD)
        scores = (
            jnp.einsum("qhd,khd->hqk", query_heads, key_tile, preferred_element_type=jnp.float32)
            * score_scale
        )
        key_index = start + jnp.arange(tile_rows, dtype=jnp.int32)
        allowed = (key_index[None, :] <= positions[:, None]) & (key_index[None, :] < valid_rows)
        return (scores, allowed[None], key_tile)

    def max_and_sum(j, carry):
        running_max, running_sum = carry
        scores, allowed, unused_tile = tile_scores(j)
        masked = jnp.where(allowed, scores, -1e30)
        new_max = jnp.maximum(running_max, jnp.max(masked, axis=-1))
        kept_terms = jnp.where(allowed, jnp.exp(masked - new_max[..., None]), 0.0)
        return (
            new_max,
            running_sum * jnp.exp(running_max - new_max) + jnp.sum(kept_terms, axis=-1),
        )

    start_stats = (
        jnp.full((H, local_rows), -1e30, jnp.float32),
        jnp.zeros((H, local_rows), jnp.float32),
    )
    running_max, running_sum = lax.fori_loop(0, tile_count, max_and_sum, start_stats)
    log_total = running_max + jnp.log(running_sum)

    def tile_probs(j):
        scores, allowed, key_tile = tile_scores(j)
        attn_probs = jnp.where(allowed, jnp.exp(scores - log_total[..., None]), 0.0)
        value_tile = lax.dynamic_slice_in_dim(value_rows, j * tile_rows, tile_rows, 0).reshape(
            tile_rows, H, HD
        )
        return (attn_probs, key_tile, value_tile)

    def accumulate(j, summed):
        attn_probs, unused_tile, value_tile = tile_probs(j)
        return summed + jnp.einsum(
            "hqk,khd->qhd",
            attn_probs.astype(jnp.bfloat16),
            value_tile,
            preferred_element_type=jnp.float32,
        )

    attended = lax.fori_loop(0, tile_count, accumulate, jnp.zeros((local_rows, H, HD), jnp.float32))
    scaled_low = (
        (attended * scales[None, :, None]).reshape(local_rows, model_width).astype(jnp.bfloat16)
    )
    attn_proj = jnp.dot(scaled_low, out_full, preferred_element_type=jnp.float32) + attn_rows[1]
    attn_normed, norm_b_pull = jax.vjp(layer_norm, attn_proj, gain_rows[1], bias_rows[1])
    residual = residual_in + attn_normed
    ffn_in, norm_c_pull = jax.vjp(layer_norm, residual, gain_rows[2], bias_rows[2])
    ffn_low = ffn_in.astype(jnp.bfloat16)
    hidden = jnp.dot(ffn_low, up_full, preferred_element_type=jnp.float32) + ffn_rows[0]
    ffn_normed, ffn_pull = jax.vjp(gelu_norm, hidden, ffn_gain, ffn_rows[1])
    ffn_out_low = ffn_normed.astype(jnp.bfloat16)
    combined = jnp.where(
        valid_mask,
        residual
        + jnp.dot(ffn_out_low, down_full, preferred_element_type=jnp.float32)
        + bias_rows[4],
        0.0,
    )
    output = combined.astype(jnp.bfloat16)[None]
    barrier_out = lax.optimization_barrier(((w_qkv, w_out, w_up, w_down), combined))
    regathered = (
        lax.all_gather(barrier_out[0][0], ("seq", "batch"), axis=0, tiled=True),
        lax.all_gather(barrier_out[0][1], ("seq", "batch"), axis=0, tiled=True),
        lax.all_gather(barrier_out[0][2], ("seq", "batch"), axis=0, tiled=True),
        lax.all_gather(barrier_out[0][3], ("seq", "batch"), axis=0, tiled=True),
    )
    qkv_full, out_full, up_full, down_full = (
        regathered[0],
        regathered[1],
        regathered[2],
        regathered[3],
    )
    cotan_rows = jnp.where(valid_mask, cotangent[0], jnp.zeros_like(cotangent[0]))
    cotan_float = cotan_rows.astype(jnp.float32)
    grad_down = contract_rows(ffn_out_low, cotan_rows)
    grad_bias_out = jnp.sum(cotan_float, axis=0)
    grad_ffn_normed = times_transposed(cotan_rows, down_full)
    grad_hidden, grad_ffn_gain, grad_ffn_shift = ffn_pull(grad_ffn_normed)
    grad_hidden_low = grad_hidden.astype(jnp.bfloat16)
    grad_up = contract_rows(ffn_low, grad_hidden_low)
    grad_ffn_bias = jnp.sum(grad_hidden_low.astype(jnp.float32), axis=0)
    grad_ffn_in = times_transposed(grad_hidden_low, up_full)
    grad_from_ffn, grad_gain_c, grad_shift_c = norm_c_pull(grad_ffn_in)
    grad_residual = cotan_float + grad_from_ffn
    grad_proj, grad_gain_b, grad_shift_b = norm_b_pull(grad_residual)
    grad_proj_low = grad_proj.astype(jnp.bfloat16)
    grad_out_bias = jnp.sum(grad_proj_low.astype(jnp.float32), axis=0)
    grad_out = contract_rows(scaled_low, grad_proj_low)
    grad_scaled = times_transposed(grad_proj_low, out_full).reshape(local_rows, H, HD)
    grad_scales = jnp.sum(grad_scaled * attended, axis=(0, 2))
    grad_heads_low = (grad_scaled * scales[None, :, None]).astype(jnp.bfloat16)
    row_delta = jnp.einsum("qhd,qhd->hq", grad_heads_low.astype(jnp.float32), attended)

    def score_grads(j):
        attn_probs, key_tile, value_tile = tile_probs(j)
        grad_probs = jnp.einsum(
            "qhd,khd->hqk", grad_heads_low, value_tile, preferred_element_type=jnp.float32
        )
        grad_scores = (attn_probs * (grad_probs - row_delta[..., None])).astype(jnp.bfloat16)
        return (attn_probs, grad_scores, key_tile)

    def backward_tile(j, carry):
        grad_query, terms = carry
        attn_probs, grad_scores, key_tile = score_grads(j)
        grad_query = grad_query + jnp.einsum(
            "hqk,khd->qhd", grad_scores, key_tile, preferred_element_type=jnp.float32
        )
        grad_key = (
            jnp.einsum("hqk,qhd->khd", grad_scores, query_heads, preferred_element_type=jnp.float32)
            * score_scale
        )
        grad_value = jnp.einsum(
            "hqk,qhd->khd",
            attn_probs.astype(jnp.bfloat16),
            grad_heads_low,
            preferred_element_type=jnp.float32,
        )
        piece = jnp.concatenate(
            [grad_key.reshape(tile_rows, model_width), grad_value.reshape(tile_rows, model_width)],
            axis=1,
        )
        return (grad_query, lax.dynamic_update_slice_in_dim(terms, piece, j * tile_rows, 0))

    start_carry = (
        jnp.zeros((local_rows, H, HD), jnp.float32),
        jnp.zeros((seq_length, 2 * model_width), jnp.float32),
    )
    grad_query, terms = lax.fori_loop(0, tile_count, backward_tile, start_carry)
    grad_kv = lax.psum_scatter(terms, "seq", scatter_dimension=0, tiled=True)
    grad_query_low = (
        (grad_query * score_scale).reshape(local_rows, model_width).astype(jnp.bfloat16)
    )
    grad_kv_low = grad_kv.astype(jnp.bfloat16)
    grad_projected = jnp.concatenate([grad_query_low, grad_kv_low], axis=1)
    grad_qkv = contract_rows(normed_low, grad_projected)
    grad_query_bias = jnp.sum(grad_query_low.astype(jnp.float32), axis=0)
    grad_value_bias = jnp.sum(grad_kv_low[:, model_width:].astype(jnp.float32), axis=0)
    grad_normed = times_transposed(grad_projected, qkv_full)
    grad_from_attn, grad_gain_a, grad_shift_a = norm_a_pull(grad_normed)
    grad_input = (grad_residual + grad_from_attn).astype(jnp.bfloat16)[None]
    reduced = (
        lax.psum_scatter(grad_qkv, ("seq", "batch"), scatter_dimension=0, tiled=True),
        lax.psum_scatter(grad_out, ("seq", "batch"), scatter_dimension=0, tiled=True),
        lax.psum_scatter(grad_up, ("seq", "batch"), scatter_dimension=0, tiled=True),
        lax.psum_scatter(grad_down, ("seq", "batch"), scatter_dimension=0, tiled=True),
        lax.psum_scatter(
            jnp.stack([grad_gain_a, grad_gain_b, grad_gain_c]),
            ("seq", "batch"),
            scatter_dimension=1,
            tiled=True,
        ),
        lax.psum_scatter(
            jnp.stack([grad_shift_a, grad_shift_b, grad_shift_c, grad_query_bias, grad_bias_out]),
            ("seq", "batch"),
            scatter_dimension=1,
            tiled=True,
        ),
        lax.psum_scatter(
            jnp.stack([grad_value_bias, grad_out_bias]),
            ("seq", "batch"),
            scatter_dimension=1,
            tiled=True,
        ),
        lax.psum_scatter(grad_ffn_gain, ("seq", "batch"), scatter_dimension=0, tiled=True),
        lax.psum_scatter(
            jnp.stack([grad_ffn_bias, grad_ffn_shift]),
            ("seq", "batch"),
            scatter_dimension=1,
            tiled=True,
        ),
    )
    scale_total = lax.psum(grad_scales, ("seq", "batch"))
    return (
        output,
        grad_input,
        reduced[0],
        reduced[1],
        reduced[2],
        reduced[3],
        reduced[4],
        reduced[5],
        reduced[6],
        reduced[7],
        reduced[8],
        scale_total,
    )


def solution(mesh):
    return jax.shard_map(
        shards,
        mesh=mesh,
        in_specs=(
            P("batch", "seq", None),
            P("batch"),
            P(("seq", "batch"), None),
            P(("seq", "batch"), None),
            P(("seq", "batch"), None),
            P(("seq", "batch"), None),
            P(None, ("seq", "batch")),
            P(None, ("seq", "batch")),
            P(None, ("seq", "batch")),
            P(("seq", "batch")),
            P(None, ("seq", "batch")),
            P(),
            P("batch", "seq", None),
        ),
        out_specs=(
            P("batch", "seq", None),
            P("batch", "seq", None),
            P(("seq", "batch"), None),
            P(("seq", "batch"), None),
            P(("seq", "batch"), None),
            P(("seq", "batch"), None),
            P(None, ("seq", "batch")),
            P(None, ("seq", "batch")),
            P(None, ("seq", "batch")),
            P(("seq", "batch")),
            P(None, ("seq", "batch")),
            P(),
        ),
        check_vma=False,
    )
```

profile of v0, /device:TPU:0, one launch (start us, length us, event | category | flops | bytes accessed | tf_op | source)
XLA Modules:
  0.0 2467.9 jit_solution(1627188962790844929)
XLA Ops:
  8.0 70.8 %all-gather = bf16[32,32,3]{1,2,0:T(4,128)(2,1)S(1)} all-gather(bf16[1,32,3]{1,2,0:T(4,128)(2,1)} %bitcast.317), channel_id=1, replica_groups=mesh['seq'=8,'batch'=4] {'seq','batch'}, dimensions={0}, use_global_device_ids=true | all-gather | bytes 6336 | tf_op jit(solution)/shard_map/all_gather | solution.py:55
  78.9 64.1 %all-gather.1 = bf16[32,32,5]{1,2,0:T(8,128)(2,1)S(1)} all-gather(bf16[1,32,5]{1,2,0:T(8,128)(2,1)} %bitcast.316), channel_id=1, replica_groups=mesh['seq'=8,'batch'=4] {'seq','batch'}, dimensions={0}, use_global_device_ids=true | all-gather | bytes 10560 | tf_op jit(solution)/shard_map/all_gather | solution.py:56
  143.1 65.8 %all-gather.2 = bf16[32,32,2]{1,2,0:T(2,128)(2,1)S(1)} all-gather(bf16[1,32,2]{1,2,0:T(2,128)(2,1)} %bitcast.318), channel_id=1, replica_groups=mesh['seq'=8,'batch'=4] {'seq','batch'}, dimensions={0}, use_global_device_ids=true | all-gather | bytes 4224 | tf_op jit(solution)/shard_map/all_gather | solution.py:57
  219.3 63.5 %all_gather.53 = bf16[2,4096]{1,0:T(2,128)(2,1)S(1)} all-gather(bf16[2,128]{1,0:T(2,128)(2,1)S(1)} %copy-done.52), channel_id=1, replica_groups=mesh['seq'=8,'batch'=4] {'seq','batch'}, dimensions={1}, use_global_device_ids=true | all-gather | bytes 16896 | tf_op jit(solution)/shard_map/all_gather | solution.py:59
  284.6 65.7 %all-gather.3 = bf16[32,1,128]{2,1,0:T(2,128)(2,1)S(1)} all-gather(bf16[1,1,128]{2,1,0:T(2,128)(2,1)S(1)} %bitcast.319), channel_id=1, replica_groups=mesh['seq'=8,'batch'=4] {'seq','batch'}, dimensions={0}, use_global_device_ids=true | all-gather | bytes 8448 | tf_op jit(solution)/shard_map/all_gather | solution.py:58
  361.9 7.4 while.38
  373.8 35.3 %all-gather.23.cloned.1.call-done = bf16[1024,4096]{1,0:T(8,128)(2,1)} async-done(((bf16[32,4096]{1,0:T(8,128)(2,1)}), bf16[1024,4096]{1,0:T(8,128)(2,1)}) %all-gather.23.cloned.1.call-update) | async-done | bytes 8388624 | tf_op jit(solution)/shard_map/all_gather | solution.py:53
  409.1 9.4 fusion.67
  420.1 67.4 %all-gather.25.cloned.1.call-done = bf16[4096,1024]{1,0:T(8,128)(2,1)} async-done(((bf16[128,1024]{1,0:T(8,128)(2,1)}), bf16[4096,1024]{1,0:T(8,128)(2,1)}) %all-gather.25.cloned.1.call-update) | async-done | bytes 8388624 | tf_op jit(solution)/shard_map/all_gather | solution.py:54
  487.6 6.1 fusion.32
  495.4 74.1 %all-gather.27.cloned.1.call-done = bf16[4096,1024]{1,0:T(8,128)(2,1)} async-done(((bf16[128,1024]{1,0:T(8,128)(2,1)}), bf16[4096,1024]{1,0:T(8,128)(2,1)}) %all-gather.27.cloned.1.call-update) | async-done | bytes 8388624 | tf_op jit(solution)/shard_map/all_gather | solution.py:166
  569.5 7.3 fusion.63
  581.7 66.5 %all-gather.29.cloned.1.call-done = bf16[1024,4096]{1,0:T(8,128)(2,1)} async-done(((bf16[32,4096]{1,0:T(8,128)(2,1)}), bf16[1024,4096]{1,0:T(8,128)(2,1)}) %all-gather.29.cloned.1.call-update) | async-done | bytes 8388624 | tf_op jit(solution)/shard_map/all_gather | solution.py:165
  648.2 7.4 multiply_reduce_fusion.4
  658.4 47.7 %all-gather.31.cloned.1.call-done = bf16[1024,1024]{1,0:T(8,128)(2,1)} async-done(((bf16[32,1024]{1,0:T(8,128)(2,1)}), bf16[1024,1024]{1,0:T(8,128)(2,1)}) %all-gather.31.cloned.1.call-update) | async-done | bytes 2097168 | tf_op jit(solution)/shard_map/all_gather | solution.py:164
  710.5 4.3 broadcast_in_dim.137
  714.9 11.9 while.39
  729.9 77.7 %reduce-scatter.18.cloned.1.call-done = f32[128,2048]{0,1:T(8,128)} async-done(((f32[1024,2048]{0,1:T(8,128)}), f32[128,2048]{0,1:T(8,128)}) %reduce-scatter.18.cloned.1.call-update) | async-done | bytes 1048592 | tf_op jit(solution)/shard_map/reduce_scatter | solution.py:230
  809.0 70.8 %all-gather.33.cloned.1.call-done = bf16[1024,3072]{1,0:T(8,128)(2,1)} async-done(((bf16[32,3072]{1,0:T(8,128)(2,1)}), bf16[1024,3072]{1,0:T(8,128)(2,1)}) %all-gather.33.cloned.1.call-update) | async-done | bytes 6291472 | tf_op jit(solution)/shard_map/all_gather | solution.py:163
  879.8 5.1 fusion.64
  893.7 9.2 fusion.60
  903.9 6.4 fusion.48
  911.5 8.2 fusion.62
  921.1 40.1 %all-reduce.1 = (f32[4096]{0:T(1024)S(1)}, f32[16]{0:T(128)}) all-reduce(f32[4096]{0:T(1024)S(1)} %get-tuple-element.367, f32[16]{0:T(128)S(1)} %multiply_reduce_fusion.3), channel_id=10, replica_groups=mesh['seq'=8,'batch'=4] {'seq','batch'}, use_global_device_ids=true, to_apply=%region_43.44.clone | all-reduce | flops 4112 | bytes 32896
  961.8 58.5 %reduce-scatter.34.cloned.1.call-done = f32[128,2]{1,0:T(8,128)} async-done(((f32[4096,2]{1,0:T(8,128)}), f32[128,2]{1,0:T(8,128)}) %reduce-scatter.34.cloned.1.call-update) | async-done | bytes 1040
  1022.8 133.6 %reduce-scatter.32.cloned.1.call-done = f32[32,2]{1,0:T(8,128)} async-done(((f32[1024,2]{1,0:T(8,128)}), f32[32,2]{1,0:T(8,128)}) %reduce-scatter.32.cloned.1.call-update) | async-done | bytes 272
  1157.8 133.1 %reduce-scatter.28.cloned.1.call-done = f32[32,3]{1,0:T(8,128)} async-done(((f32[1024,3]{1,0:T(8,128)}), f32[32,3]{1,0:T(8,128)}) %reduce-scatter.28.cloned.1.call-update) | async-done | bytes 400
  1292.2 133.0 %reduce-scatter.30.cloned.1.call-done = f32[32,5]{1,0:T(8,128)} async-done(((f32[1024,5]{1,0:T(8,128)}), f32[32,5]{1,0:T(8,128)}) %reduce-scatter.30.cloned.1.call-update) | async-done | bytes 656
  1426.6 146.1 %reduce-scatter.22.cloned.1.call-done = f32[32,1024]{1,0:T(8,128)} async-done(((f32[1024,1024]{1,0:T(8,128)}), f32[32,1024]{1,0:T(8,128)}) %reduce-scatter.22.cloned.1.call-update) | async-done | bytes 131088 | tf_op jit(solution)/shard_map/reduce_scatter | solution.py:244
  1572.7 363.2 %reduce-scatter.26.cloned.1.call-done = f32[128,1024]{1,0:T(8,128)} async-done(((f32[4096,1024]{1,0:T(8,128)}), f32[128,1024]{1,0:T(8,128)}) %reduce-scatter.26.cloned.1.call-update) | async-done | bytes 524304 | tf_op jit(solution)/shard_map/reduce_scatter | solution.py:246
  1936.0 162.6 %reduce-scatter.20.cloned.1.call-done = f32[32,3072]{1,0:T(8,128)} async-done(((f32[1024,3072]{1,0:T(8,128)}), f32[32,3072]{1,0:T(8,128)}) %reduce-scatter.20.cloned.1.call-update) | async-done | bytes 393232 | tf_op jit(solution)/shard_map/reduce_scatter | solution.py:243
  2098.6 362.5 %reduce-scatter.24.cloned.1.call-done = f32[32,4096]{1,0:T(8,128)} async-done(((f32[1024,4096]{1,0:T(8,128)}), f32[32,4096]{1,0:T(8,128)}) %reduce-scatter.24.cloned.1.call-update) | async-done | bytes 524304 | tf_op jit(solution)/shard_map/reduce_scatter | solution.py:245
  (271 shorter events, 88.7 us)
Async XLA Ops:
  7.2 204.7 %all-gather.15.cloned.1.call-start = ((), (), s32[]{:S(2)}) async-start(), calls=%async_computation.9 | async-start | bytes 6488064 | tf_op jit(solution)/shard_map/all_gather | solution.py:51
  7.9 343.2 %all-gather.19.cloned.1.call-start = ((), (), s32[]{:S(2)}) async-start(), calls=%async_computation.11 | async-start | bytes 2359296 | tf_op jit(solution)/shard_map/all_gather | solution.py:88
  215.9 68.2 %copy-start.58 = (bf16[16]{0:T(256)(128)(2,1)S(1)}, bf16[16]{0:T(256)(128)(2,1)}, u32[]{:S(2)}) copy-start(bf16[16]{0:T(256)(128)(2,1)} %param.30) | copy-start | bytes 100
  215.9 68.7 %copy-start.53 = (bf16[128]{0:T(256)(128)(2,1)S(1)}, bf16[128]{0:T(256)(128)(2,1)}, u32[]{:S(2)}) copy-start(bf16[128]{0:T(256)(128)(2,1)} %param.28) | copy-start | bytes 772
  216.8 137.2 %all-gather.17.cloned.1.call-start = ((), (), s32[]{:S(2)}) async-start(), calls=%async_computation.10 | async-start | bytes 2359296 | tf_op jit(solution)/shard_map/all_gather | solution.py:89
  217.5 153.0 %all-gather.21.cloned.1.call-start = ((), (), s32[]{:S(2)}) async-start(), calls=%async_computation.12 | async-start | bytes 2162688 | tf_op jit(solution)/shard_map/all_gather | solution.py:52
  218.1 191.0 %all-gather.23.cloned.1.call-start = ((), (), s32[]{:S(2)}) async-start(), calls=%async_computation.13 | async-start | bytes 8650752 | tf_op jit(solution)/shard_map/all_gather | solution.py:53
  218.7 268.9 %all-gather.25.cloned.1.call-start = ((), (), s32[]{:S(2)}) async-start(), calls=%async_computation.14 | async-start | bytes 8650752 | tf_op jit(solution)/shard_map/all_gather | solution.py:54
  219.2 350.3 %all-gather.27.cloned.1.call-start = ((), (), s32[]{:S(2)}) async-start(), calls=%async_computation.15 | async-start | bytes 8650752 | tf_op jit(solution)/shard_map/all_gather | solution.py:166
  373.5 282.1 %copy-start.40 = (f32[128]{0:T(128)}, f32[128]{0:T(128)S(1)}, u32[]{:S(2)}) copy-start(f32[128]{0:T(128)S(1)} %broadcast_multiply_fusion.1) | copy-start | bytes 1540
  373.7 281.9 %copy-start.44 = (f32[128]{0:T(128)}, f32[128]{0:T(128)S(1)}, u32[]{:S(2)}) copy-start(f32[128]{0:T(128)S(1)} %fusion.53) | copy-start | bytes 1540
  418.4 69.1 %copy-start.42 = (pred[128]{0:T(512)(128)(4,1)S(1)}, pred[128]{0:T(512)(128)(4,1)}, u32[]{:S(2)}) copy-start(pred[128]{0:T(512)(128)(4,1)} %add_compare_fusion) | copy-start | bytes 388
  420.1 157.6 %copy-start.31 = (f32[128]{0:T(128)}, f32[128]{0:T(128)S(1)}, u32[]{:S(2)}) copy-start(f32[128]{0:T(128)S(1)} %fusion.54) | copy-start | bytes 1540
  487.6 82.0 %copy-start.14 = (bf16[1,128,1024]{2,1,0:T(8,128)(2,1)S(1)}, bf16[1,128,1024]{2,1,0:T(8,128)(2,1)}, u32[]{:S(2)}) copy-start(bf16[1,128,1024]{2,1,0:T(8,128)(2,1)} %param.31) | copy-start | bytes 786436
  493.7 154.5 %all-gather.29.cloned.1.call-start = ((), (), s32[]{:S(2)}) async-start(), calls=%async_computation.16 | async-start | bytes 8650752 | tf_op jit(solution)/shard_map/all_gather | solution.py:165
  494.4 211.7 %all-gather.31.cloned.1.call-start = ((), (), s32[]{:S(2)}) async-start(), calls=%async_computation.17 | async-start | bytes 2162688 | tf_op jit(solution)/shard_map/all_gather | solution.py:164
  495.2 312.4 %reduce-scatter.18.cloned.1.call-start = ((), (), s32[]{:S(2)}) async-start(), calls=%async_computation.18 | async-start | bytes 9437184 | tf_op jit(solution)/shard_map/reduce_scatter | solution.py:230
  726.8 153.0 %all-gather.33.cloned.1.call-start = ((), (), s32[]{:S(2)}) async-start(), calls=%async_computation.19 | async-start | bytes 6488064 | tf_op jit(solution)/shard_map/all_gather | solution.py:163
  727.5 292.8 %reduce-scatter.34.cloned.1.call-start = ((), (), s32[]{:S(2)}) async-start(), calls=%async_computation.27 | async-start | bytes 2162688
  729.8 150.0 %copy-start.25 = (bf16[128,16,64]{0,2,1:T(8,128)(2,1)}, bf16[128,16,64]{0,2,1:T(8,128)(2,1)S(1)}, u32[]{:S(2)}) copy-start(bf16[128,16,64]{0,2,1:T(8,128)(2,1)S(1)} %get-tuple-element.446) | copy-start | bytes 786436
  729.8 150.0 %copy-start.5 = (bf16[1,128,1024]{2,1,0:T(8,128)(2,1)S(1)}, bf16[1,128,1024]{2,1,0:T(8,128)(2,1)}, u32[]{:S(2)}) copy-start(bf16[1,128,1024]{2,1,0:T(8,128)(2,1)} %param.19) | copy-start | bytes 786436
  729.8 426.6 %reduce-scatter.32.cloned.1.call-start = ((), (), s32[]{:S(2)}) async-start(), calls=%async_computation.26 | async-start | bytes 540672
  886.9 403.9 %reduce-scatter.28.cloned.1.call-start = ((), (), s32[]{:S(2)}) async-start(), calls=%async_computation.24 | async-start | bytes 540672
  888.1 537.1 %reduce-scatter.30.cloned.1.call-start = ((), (), s32[]{:S(2)}) async-start(), calls=%async_computation.25 | async-start | bytes 540672
  889.4 683.3 %reduce-scatter.22.cloned.1.call-start = ((), (), s32[]{:S(2)}) async-start(), calls=%async_computation.21 | async-start | bytes 4325376 | tf_op jit(solution)/shard_map/reduce_scatter | solution.py:244
  892.1 1043.8 %reduce-scatter.26.cloned.1.call-start = ((), (), s32[]{:S(2)}) async-start(), calls=%async_computation.23 | async-start | bytes 17301504 | tf_op jit(solution)/shard_map/reduce_scatter | solution.py:246
  902.9 1195.6 %reduce-scatter.20.cloned.1.call-start = ((), (), s32[]{:S(2)}) async-start(), calls=%async_computation.20 | async-start | bytes 12976128 | tf_op jit(solution)/shard_map/reduce_scatter | solution.py:243
  910.3 1550.8 %reduce-scatter.24.cloned.1.call-start = ((), (), s32[]{:S(2)}) async-start(), calls=%async_computation.22 | async-start | bytes 17301504 | tf_op jit(solution)/shard_map/reduce_scatter | solution.py:245
  919.7 102.1 %copy-start.51 = (f32[128]{0:T(128)S(1)}, f32[128]{0:T(128)}, u32[]{:S(2)}) copy-start(f32[128]{0:T(128)} %get-tuple-element.376) | copy-start | bytes 1540
  919.7 102.1 %copy-start.13 = (f32[128,1024]{1,0:T(8,128)S(1)}, f32[128,1024]{1,0:T(8,128)}, u32[]{:S(2)}) copy-start(f32[128,1024]{1,0:T(8,128)} %copy-done.12) | copy-start | bytes 1572868
  919.7 102.1 %copy-start.21 = (f32[128,1024]{1,0:T(8,128)S(1)}, f32[128,1024]{1,0:T(8,128)}, u32[]{:S(2)}) copy-start(f32[128,1024]{1,0:T(8,128)} %copy-done.20) | copy-start | bytes 1572868
  919.7 102.1 %copy-start.47 = (f32[128]{0:T(128)S(1)}, f32[128]{0:T(128)}, u32[]{:S(2)}) copy-start(f32[128]{0:T(128)} %copy-done.46) | copy-start | bytes 1540
  (48 other events, 329.4 us)
Sparse Core Ops, SparseCore 0:
  10.9 72.1 all-gather.14
  216.9 23.9 all-gather.18
  243.3 27.7 all-gather.16
  273.9 56.3 all-gather.20
  333.1 75.9 all-gather.22
  411.8 75.6 all-gather.24
  493.8 75.6 all-gather.26
  572.5 75.7 all-gather.28
  651.2 54.9 all-gather.30
  726.9 80.6 reduce-scatter.17
  810.5 69.2 all-gather.32
  881.9 138.3 reduce-scatter.33
  1022.6 133.8 reduce-scatter.31
  1158.5 132.3 reduce-scatter.27
  1292.9 132.2 reduce-scatter.29
  1428.0 144.7 reduce-scatter.21
  1575.4 360.4 reduce-scatter.25
  1942.4 156.1 reduce-scatter.19
  2101.4 359.6 reduce-scatter.23
where the time goes:
time: 2470 us
  waiting for transfers between devices  1940 us (79%)
  blocking collectives  370 us (15%)
  matrix products  80.5 us (3%)
  local copies, waits for them, and re-layouts  41.6 us (2%)
    unnamed x23, waiting for transfers between devices  463 us
    reduce_scatter x1, waiting for transfers between devices, shards(): lax.psum_scatter(grad_down, ('seq', 'batch'), scatter_dimension=0, tiled=...  363 us
    reduce_scatter x1, waiting for transfers between devices, shards(): lax.psum_scatter(grad_up, ('seq', 'batch'), scatter_dimension=0, tiled=True)  363 us
    reduce_scatter x1, waiting for transfers between devices, shards(): lax.psum_scatter(grad_qkv, ('seq', 'batch'), scatter_dimension=0, tiled=T...  163 us
    reduce_scatter x1, waiting for transfers between devices, shards(): lax.psum_scatter(grad_out, ('seq', 'batch'), scatter_dimension=0, tiled=T...  146 us
    reduce_scatter x1, waiting for transfers between devices, shards(): grad_kv = lax.psum_scatter(terms, 'seq', scatter_dimension=0, tiled=True)  77.7 us
    all_gather x1, waiting for transfers between devices, shards(): lax.all_gather(barrier_out[0][3], ('seq', 'batch'), axis=0, tiled=True)  74.1 us
    all_gather x1, blocking collectives, shards(): lax.all_gather(norm_gains, ('seq', 'batch'), axis=1, tiled=True)  70.8 us
  transfers between devices with their start and end apart: 19, of which 15 were waited for; matrix products, arithmetic and copies ran while one was open for 4% of the time, Pallas kernels for 0%

commit v1 on v0

--- a/solution.py
+++ b/solution.py
@@ -1,6 +1,8 @@
 import jax
 import jax.numpy as jnp
 from jax import lax
+from jax.experimental import pallas as pl
+from jax.experimental.pallas import tpu as pltpu
 from jax.sharding import PartitionSpec as P
 
 H = 16
@@ -287,9 +289,659 @@
     )
 
 
+BF = jnp.bfloat16
+F32 = jnp.float32
+
+
+class Exchange:
+    def __init__(self, send_sems, recv_sems, local_sems):
+        self.send_sems = send_sems
+        self.recv_sems = recv_sems
+        self.local_sems = local_sems
+        self.count = 0
+        self.locals = 0
+        self.sent = []
+        self.s = lax.axis_index("seq")
+        self.b = lax.axis_index("batch")
+        self.chip = self.s // 2
+        self.core = self.s % 2
+        self.sibling = self.chip * 2 + 1 - self.core
+
+    def send(self, src, dst, seq, batch):
+        at = self.count
+        self.count += 1
+        copy = pltpu.make_async_remote_copy(
+            src_ref=src,
+            dst_ref=dst,
+            send_sem=self.send_sems.at[at],
+            recv_sem=self.recv_sems.at[at],
+            device_id=(seq, batch),
+            device_id_type=pl.DeviceIdType.MESH,
+        )
+        copy.start()
+        self.sent.append(copy)
+        return copy
+
+    def local(self, src, dst):
+        at = self.locals
+        self.locals += 1
+        copy = pltpu.make_async_copy(src, dst, self.local_sems.at[at])
+        copy.start()
+        return copy
+
+    def arrived(self, copies):
+        for copy in copies:
+            copy.wait_recv()
+
+    def finish(self):
+        for copy in self.sent:
+            copy.wait_send()
+
+    def peer(self, k):
+        return ((self.chip + k) % 4) * 2 + self.core
+
+    def source(self, k):
+        return ((self.chip + 4 - k) % 4) * 2 + self.core
+
+    def plane(self):
+        return [(self.s + j) % 8 for j in range(1, 8)]
+
+    def line(self):
+        return [(self.b + k) % 4 for k in range(1, 4)]
+
+    def gather_start(self, src, slot):
+        copies = [self.send(src, slot(self.s), self.peer(k), self.b) for k in (1, 2, 3)]
+        copies.append(self.send(src, slot(self.s), self.sibling, self.b))
+        return copies
+
+    def gather_forward(self, copies, slot):
+        passed = []
+        for k in (1, 2, 3):
+            copies[k - 1].wait_recv()
+            came = slot(self.source(k))
+            passed.append(self.send(came, came, self.sibling, self.b))
+        return [copies[3]] + passed
+
+    def sum_pair(self, src, from_pair):
+        return [
+            self.send(src.at[((self.chip + k) % 4) * 2 + 1 - self.core], from_pair.at[k], self.sibling, self.b)
+            for k in (1, 2, 3, 0)
+        ]
+
+    def sum_chips(self, copies, src, from_pair, paired, from_chips, total):
+        over = []
+        for at, k in enumerate((1, 2, 3, 0)):
+            copies[at].wait_recv()
+            mine = src[((self.chip + k) % 4) * 2 + self.core].astype(F32)
+            both = mine + from_pair[k].astype(F32)
+            if k:
+                paired[k - 1] = both.astype(BF)
+                over.append(self.send(paired.at[k - 1], from_chips.at[k - 1], self.peer(k), self.b))
+            else:
+                total[...] = both
+        return over
+
+    def sum_end(self, over, from_chips, total):
+        self.arrived(over)
+        return total[...] + from_chips[0].astype(F32) + from_chips[1].astype(F32) + from_chips[2].astype(F32)
+
+
+def columns(start, size):
+    return pl.ds(pl.multiple_of(start, 128), size)
+
+
+def centred(rows):
+    middle = rows - jnp.mean(rows, axis=-1, keepdims=True)
+    inverse = lax.rsqrt(jnp.mean(middle * middle, axis=-1, keepdims=True) + NORM_EPSILON)
+    return middle * inverse, inverse
+
+
+def norm_back(upstream, gain, normal, inverse):
+    scaled = upstream * gain
+    average = jnp.mean(scaled, axis=-1, keepdims=True)
+    along = jnp.mean(scaled * normal, axis=-1, keepdims=True)
+    return inverse * (scaled - average - normal * along)
+
+
+def gelu_parts(z):
+    phi = 0.5 * (1.0 + lax.erf(z * 0.7071067811865476))
+    density = 0.3989422804014327 * jnp.exp(-0.5 * z * z)
+    return z * phi, phi + z * density
+
+
+def matmul(left, right):
+    return jnp.dot(left, right, preferred_element_type=F32)
+
+
+def column_sum(rows):
+    return jnp.sum(rows, axis=0, keepdims=True)
+
+
+def pack_columns(parts):
+    lane = lax.broadcasted_iota(jnp.int32, (128, 128), 1)
+    wide = jnp.zeros((128, 128), F32)
+    for at, part in enumerate(parts):
+        wide = jnp.where(lane == at, part, wide)
+    return wide.T[:8]
+
+
+BUFFERS = dict(
+    x_all=((8, 128, 1024), BF),
+    g_all=((8, 128, 1024), BF),
+    qkv_w=((8, 4, 32, 384), BF),
+    out_w=((8, 4, 32, 1024), BF),
+    up_w=((8, 4, 32, 512), BF),
+    down_w=((4, 128, 1024), BF),
+    vec_all=((32, 16, 128), F32),
+    rows=((16, 1024), F32),
+    ff_rows=((8, 512), F32),
+    h1=((1024, 1024), BF),
+    qkv=((1024, 384), BF),
+    probs_low=((2, 512, 512), F32),
+    probs_high=((2, 512, 1024), F32),
+    attended=((1024, 128), F32),
+    scaled=((8, 128, 128), BF),
+    scaled_local=((128, 1024), BF),
+    normal_b=((128, 1024), F32),
+    normal_c=((128, 1024), F32),
+    residual=((128, 1024), F32),
+    h2_all=((8, 128, 1024), BF),
+    active=((1024, 512), F32),
+    slope=((1024, 512), F32),
+    du2=((1024, 512), F32),
+    stats=((8, 8, 128), F32),
+    stats_all=((8, 8, 8, 128), F32),
+    u2=((1024, 512), BF),
+    dz=((1024, 512), BF),
+    dh2_src=((8, 128, 1024), BF),
+    dh2_pair=((4, 128, 1024), BF),
+    dh2_paired=((3, 128, 1024), BF),
+    dh2_chips=((3, 128, 1024), BF),
+    ffo_src=((8, 128, 1024), BF),
+    ffo_pair=((4, 128, 1024), BF),
+    ffo_paired=((3, 128, 1024), BF),
+    ffo_chips=((3, 128, 1024), BF),
+    dh1_src=((8, 128, 1024), BF),
+    dh1_pair=((4, 128, 1024), BF),
+    dh1_paired=((3, 128, 1024), BF),
+    dh1_chips=((3, 128, 1024), BF),
+    total=((128, 1024), F32),
+    ffo_total=((128, 1024), F32),
+    dr=((128, 1024), F32),
+    da_all=((8, 128, 1024), BF),
+    do_local=((128, 1024), BF),
+    do_all=((8, 128, 128), BF),
+    dq=((1024, 128), F32),
+    dk=((1024, 128), F32),
+    dv=((1024, 128), F32),
+    dqkv=((1024, 384), BF),
+    up_src=((8, 4, 32, 512), BF),
+    up_terms=((4, 8, 32, 512), BF),
+    down_src=((4, 128, 1024), BF),
+    down_terms=((4, 128, 1024), BF),
+    qkv_src=((8, 4, 32, 384), BF),
+    qkv_terms=((4, 8, 32, 384), BF),
+    out_src=((4, 32, 1024), BF),
+    out_terms=((4, 32, 1024), BF),
+    up_own=((8, 32, 512), BF),
+    up_fin=((32, 4096), BF),
+    qkv_own=((8, 32, 384), BF),
+    qkv_fin=((32, 3072), BF),
+    close_src=((8, 16, 128), F32),
+    close_all=((32, 16, 128), F32),
+    ff_src=((4, 8, 128), F32),
+    ff_all=((4, 8, 128), F32),
+)
+COPIES = 240
+INPUTS = 9
+OUTPUTS = 8
+
+
+def block_kernel(length_in, x_in, g_in, qkv_in, out_in, up_in, down_in, vec_in, scale_in, *refs):
+    output, grad_input, grad_qkv, grad_out, grad_up, grad_down, vec_out, ff_out = refs[:OUTPUTS]
+    B = type("Buffers", (), dict(zip(BUFFERS, refs[OUTPUTS : OUTPUTS + len(BUFFERS)])))
+    ex = Exchange(*refs[OUTPUTS + len(BUFFERS) :])
+    s, b = ex.s, ex.b
+    me = s * 4 + b
+    valid_rows = length_in[0, 0]
+
+    barrier = pltpu.get_barrier_semaphore()
+    partners = [((s + j // 4) % 8, (b + j % 4) % 4) for j in range(1, 32)]
+    for seq, batch in partners:
+        pl.semaphore_signal(barrier, inc=1, device_id=(seq, batch), device_id_type=pl.DeviceIdType.MESH)
+    pl.semaphore_wait(barrier, len(partners))
+
+    qkv_part = lambda p, t: qkv_in.at[:, columns(t * 1024 + p * 128, 128)]
+    qkv_slot = lambda t: B.qkv_w.at[s, b, :, pl.ds(t * 128, 128)]
+    qkv_copies = [ex.send(qkv_part(p, t), qkv_slot(t), p, b) for p in ex.plane() for t in range(3)]
+    own = [ex.local(qkv_part(s, t), qkv_slot(t)) for t in range(3)]
+    own_up = ex.local(up_in.at[:, columns(s * 512, 512)], B.up_w.at[s, b])
+    own_rest = [
+        ex.local(out_in, B.out_w.at[s, b]),
+        ex.local(x_in, B.x_all.at[s]),
+        ex.local(g_in, B.g_all.at[s]),
+        ex.local(down_in, B.down_w.at[b]),
+        ex.local(vec_in, B.vec_all.at[me]),
+    ]
+    x_slot = lambda i: B.x_all.at[i]
+    g_slot = lambda i: B.g_all.at[i]
+    x_copies = ex.gather_start(x_in, x_slot)
+    vec_copies = [ex.send(vec_in, B.vec_all.at[me], p, q) for p, q in partners]
+    up_copies = [ex.send(up_in.at[:, columns(p * 512, 512)], B.up_w.at[s, b], p, b) for p in ex.plane()]
+    ex.arrived(qkv_copies)
+    for one in own:
+        one.wait()
+    qkv_line = [ex.send(B.qkv_w.at[:, b], B.qkv_w.at[:, b], s, q) for q in ex.line()]
+    out_line = [ex.send(out_in, B.out_w.at[s, b], s, q) for q in ex.line()]
+    down_line = [ex.send(down_in, B.down_w.at[b], s, q) for q in ex.line()]
+    x_passed = ex.gather_forward(x_copies, x_slot)
+    g_copies = ex.gather_start(g_in, g_slot)
+    ex.arrived(up_copies)
+    own_up.wait()
+    up_line = [ex.send(B.up_w.at[:, b], B.up_w.at[:, b], s, q) for q in ex.line()]
+    ex.arrived(vec_copies)
+    for one in own_rest:
+        one.wait()
+
+    for p in range(8):
+        group = B.vec_all[4 * p] + B.vec_all[4 * p + 1] + B.vec_all[4 * p + 2] + B.vec_all[4 * p + 3]
+        B.rows[:, p * 128 : (p + 1) * 128] = group
+    for q in range(4):
+        B.ff_rows[:, q * 128 : (q + 1) * 128] = B.vec_all[s * 4 + q][8:16]
+    row = lambda at: B.rows[at : at + 1, :]
+    gain_a, gain_b, gain_c = row(0), row(1), row(2)
+    bias_a, bias_b, bias_c, bias_out, bias_attn = row(3), row(4), row(5), row(7), row(9)
+    ffn_gain, ffn_bias, ffn_shift = B.ff_rows[2:3, :], B.ff_rows[3:4, :], B.ff_rows[4:5, :]
+    own_columns = columns(s * 128, 128)
+    query_bias = B.rows[6:7, own_columns]
+    value_bias = B.rows[8:9, own_columns]
+    own_scale = scale_in[0:1, own_columns]
+
+    ex.arrived(x_passed)
+
+    @pl.loop(0, 8)
+    def _(t):
+        normal, _unused = centred(B.x_all[t].astype(F32))
+        B.h1[pl.ds(t * 128, 128), :] = (normal * gain_a + bias_a).astype(BF)
+
+    ex.arrived(qkv_line)
+    offsets = jnp.concatenate([query_bias, jnp.zeros_like(query_bias), value_bias], axis=1)
+
+    @pl.loop(0, 4)
+    def _(t):
+        at = pl.ds(t * 256, 256)
+        B.qkv[at, :] = (matmul(B.h1[at, :], B.qkv_w[...].reshape(1024, 384)) + offsets).astype(BF)
+
+    ex.arrived(out_line)
+    out_slot = lambda i: B.out_w.at[i]
+    out_copies = ex.gather_start(B.out_w.at[s], out_slot)
+    g_passed = ex.gather_forward(g_copies, g_slot)
+
+    score_scale = HD ** (-0.5)
+    half_of = lax.broadcasted_iota(jnp.int32, (1, 128), 1) // HD
+
+    def of_head(rows, h):
+        return jnp.where(half_of == h, rows, jnp.zeros_like(rows))
+
+    for size in (512, 1024):
+        for h in range(2):
+
+            @pl.loop(size // 128 - 4, size // 128)
+            def _(t):
+                at = pl.ds(t * 128, 128)
+                scores = times_transposed(of_head(B.qkv[at, 0:128], h), B.qkv[0:size, 128:256]) * score_scale
+                key_index = lax.broadcasted_iota(jnp.int32, (128, size), 1)
+                query_index = t * 128 + lax.broadcasted_iota(jnp.int32, (128, size), 0)
+                allowed = (key_index <= query_index) & (key_index < valid_rows)
+                masked = jnp.where(allowed, scores, -1e30)
+                raised = jnp.exp(masked - jnp.max(masked, axis=-1, keepdims=True))
+                probs = raised * (1.0 / jnp.sum(raised, axis=-1, keepdims=True))
+                kept = B.probs_low if size == 512 else B.probs_high
+                kept[h, pl.ds(t * 128 - size + 512, 128), :] = probs
+                found = matmul(probs.astype(BF), of_head(B.qkv[0:size, 256:384], h))
+                if h == 0:
+                    B.attended[at, :] = found
+                else:
+                    both = B.attended[at, :] + found
+                    B.attended[at, :] = both
+                    B.scaled[t] = (both * own_scale).astype(BF)
+
+    local_lanes = B.scaled_local.at[:, own_columns]
+    heads = [ex.send(B.scaled.at[p], local_lanes, p, b) for p in ex.plane()]
+    own_heads = ex.local(B.scaled.at[s], local_lanes)
+    out_passed = ex.gather_forward(out_copies, out_slot)
+    ex.arrived(out_passed)
+    ex.arrived(heads)
+    own_heads.wait()
+
+    attn_proj = matmul(B.scaled_local[...], B.out_w[...].reshape(1024, 1024)) + bias_attn
+    normal_b, inverse_b = centred(attn_proj)
+    B.normal_b[...] = normal_b
+    residual = x_in[...].astype(F32) + normal_b * gain_b + bias_b
+    B.residual[...] = residual
+    normal_c, inverse_c = centred(residual)
+    B.normal_c[...] = normal_c
+    B.h2_all[s] = (normal_c * gain_c + bias_c).astype(BF)
+    h2_slot = lambda i: B.h2_all.at[i]
+    h2_copies = ex.gather_start(B.h2_all.at[s], h2_slot)
+
+    ex.arrived(g_passed)
+    ex.arrived(down_line)
+
+    @pl.loop(0, 8)
+    def _(t):
+        B.du2[pl.ds(t * 128, 128), :] = times_transposed(B.g_all[t], B.down_w[...].reshape(512, 1024))
+
+    h2_passed = ex.gather_forward(h2_copies, h2_slot)
+    ex.arrived(up_line)
+    ex.arrived(h2_passed)
+
+    @pl.loop(0, 8)
+    def _(t):
+        at = pl.ds(t * 128, 128)
+        hidden = matmul(B.h2_all[t], B.up_w[...].reshape(1024, 512)) + ffn_bias
+        active, slope = gelu_parts(hidden)
+        B.active[at, :] = active
+        B.slope[at, :] = slope
+        dgain = B.du2[at, :] * ffn_gain
+        mean = jnp.mean(active, axis=-1, keepdims=True)
+        off = active - mean
+        add = lambda rows: jnp.sum(rows, axis=-1, keepdims=True)
+        B.stats[t] = pack_columns([mean, add(off * off), add(dgain), add(dgain * off)])
+
+    stats_copies = [ex.send(B.stats, B.stats_all.at[s], p, b) for p in ex.plane()]
+    own_stats = ex.local(B.stats, B.stats_all.at[s])
+    ex.arrived(stats_copies)
+    own_stats.wait()
+
+    def finish_hidden(t, sums):
+        at = pl.ds(t * 128, 128)
+        means = [B.stats_all[i, t, 0:1, :] for i in range(8)]
+        squares = [B.stats_all[i, t, 1:2, :] for i in range(8)]
+        firsts = [B.stats_all[i, t, 2:3, :] for i in range(8)]
+        seconds = [B.stats_all[i, t, 3:4, :] for i in range(8)]
+        mean = sum(means) * 0.125
+        shifts = [one - mean for one in means]
+        spread = (sum(squares) + 512.0 * sum(one * one for one in shifts)) * (1.0 / 4096.0)
+        inverse = lax.rsqrt(spread + NORM_EPSILON)
+        average = sum(firsts) * (1.0 / 4096.0)
+        along = inverse * sum(two + one * first for two, one, first in zip(seconds, shifts, firsts)) * (1.0 / 4096.0)
+        packed = jnp.concatenate([mean, inverse, average, along, jnp.zeros((124, 128), F32)], axis=0).T
+        mean, inverse, average, along = (packed[:, i : i + 1] for i in range(4))
+        normal = (B.active[at, :] - mean) * inverse
+        B.u2[at, :] = (normal * ffn_gain + ffn_shift).astype(BF)
+        du2 = B.du2[at, :]
+        dz = (inverse * (du2 * ffn_gain - average - normal * along) * B.slope[at, :]).astype(BF)
+        B.dz[at, :] = dz
+        B.dh2_src[t] = times_transposed(dz, B.up_w[...].reshape(1024, 512)).astype(BF)
+        return (
+            sums[0] + column_sum(du2 * normal),
+            sums[1] + column_sum(dz.astype(F32)),
+            sums[2] + column_sum(du2),
+        )
+
+    nothing = jnp.zeros((1, 512), F32)
+    ff_sums = lax.fori_loop(0, 8, finish_hidden, (nothing, nothing, nothing))
+    dh2_pairs = ex.sum_pair(B.dh2_src, B.dh2_pair)
+
+    @pl.loop(0, 8)
+    def _(t):
+        B.ffo_src[t] = matmul(B.u2[pl.ds(t * 128, 128), :], B.down_w[...].reshape(512, 1024)).astype(BF)
+
+    dh2_over = ex.sum_chips(dh2_pairs, B.dh2_src, B.dh2_pair, B.dh2_paired, B.dh2_chips, B.total)
+    ffo_pairs = ex.sum_pair(B.ffo_src, B.ffo_pair)
+
+    @pl.loop(0, 4)
+    def _(q):
+        terms = contract_rows(B.u2[:, columns(q * 128, 128)], B.g_all[...].reshape(1024, 1024))
+        B.down_src[q] = terms.astype(BF)
+
+    down_copies = [ex.send(B.down_src.at[q], B.down_terms.at[b], s, q) for q in ex.line()]
+
+    @pl.loop(0, 8)
+    def _(c):
+        rows = B.h2_all[:, :, columns(c * 128, 128)].reshape(1024, 128)
+        B.up_src[c] = contract_rows(rows, B.dz[...]).astype(BF).reshape(4, 32, 512)
+
+    up_grads = [ex.send(B.up_src.at[:, q], B.up_terms.at[b], s, q) for q in ex.line()]
+
+    dh2 = ex.sum_end(dh2_over, B.dh2_chips, B.total)
+    sum_gain_c = column_sum(dh2 * B.normal_c[...])
+    sum_shift_c = column_sum(dh2)
+    held = s * 128 + lax.broadcasted_iota(jnp.int32, (128, 1), 0) < valid_rows
+    g_local = g_in[...].astype(F32)
+    dr = g_local + norm_back(dh2, gain_c, B.normal_c[...], inverse_c)
+    B.dr[...] = dr
+    da = norm_back(dr, gain_b, B.normal_b[...], inverse_b).astype(BF)
+    B.da_all[s] = da
+    B.do_local[...] = (times_transposed(da, B.out_w[...].reshape(1024, 1024)) * scale_in[0:1, :]).astype(BF)
+    do_copies = [ex.send(B.do_local.at[:, columns(p * 128, 128)], B.do_all.at[s], p, b) for p in ex.plane()]
+    own_do = ex.local(B.do_local.at[:, own_columns], B.do_all.at[s])
+    da_slot = lambda i: B.da_all.at[i]
+    da_copies = ex.gather_start(B.da_all.at[s], da_slot)
+    ffo_over = ex.sum_chips(ffo_pairs, B.ffo_src, B.ffo_pair, B.ffo_paired, B.ffo_chips, B.ffo_total)
+    sum_gain_b = column_sum(dr * B.normal_b[...])
+    sum_shift_b = column_sum(dr)
+    sum_g = column_sum(g_local)
+    sum_da = column_sum(da.astype(F32))
+    B.dk[...] = jnp.zeros((1024, 128), F32)
+    B.dv[...] = jnp.zeros((1024, 128), F32)
+    ex.arrived(do_copies)
+    own_do.wait()
+
+    scale_sums = jnp.zeros((1, 128), F32)
+    for size in (512, 1024):
+        for h in range(2):
+
+            def back(t, sums, size=size, h=h):
+                at = pl.ds(t * 128, 128)
+                do = of_head(B.do_all[t], h)
+                along = do.astype(F32) * B.attended[at, :]
+                delta = jnp.sum(along, axis=-1, keepdims=True)
+                kept = B.probs_low if size == 512 else B.probs_high
+                probs = kept[h, pl.ds(t * 128 - size + 512, 128), :]
+                dp = times_transposed(do, B.qkv[0:size, 256:384])
+                ds = (probs * (dp - delta)).astype(BF)
+                found = matmul(ds, of_head(B.qkv[0:size, 128:256], h))
+                if h == 0:
+                    B.dq[at, :] = found
+                else:
+                    B.dq[at, :] += found
+                B.dk[0:size, :] += contract_rows(ds, of_head(B.qkv[at, 0:128], h))
+                B.dv[0:size, :] += contract_rows(probs.astype(BF), do)
+                return sums + column_sum(along)
+
+            scale_sums = lax.fori_loop(size // 128 - 4, size // 128, back, scale_sums)
+
+    def join(t, sums):
+        at = pl.ds(t * 128, 128)
+        dq = (B.dq[at, :] * score_scale).astype(BF)
+        dk = (B.dk[at, :] * score_scale).astype(BF)
+        dv = B.dv[at, :].astype(BF)
+        B.dqkv[at, 0:128] = dq
+        B.dqkv[at, 128:256] = dk
+        B.dqkv[at, 256:384] = dv
+        B.dh1_src[t] = times_transposed(B.dqkv[at, :], B.qkv_w[...].reshape(1024, 384)).astype(BF)
+        return (sums[0] + column_sum(dq.astype(F32)), sums[1] + column_sum(dv.astype(F32)))
+
+    blank = jnp.zeros((1, 128), F32)
+    sum_dq, sum_dv = lax.fori_loop(0, 8, join, (blank, blank))
+    dh1_pairs = ex.sum_pair(B.dh1_src, B.dh1_pair)
+
+    @pl.loop(0, 8)
+    def _(c):
+        terms = contract_rows(B.h1[:, columns(c * 128, 128)], B.dqkv[...])
+        B.qkv_src[c] = terms.astype(BF).reshape(4, 32, 384)
+
+    qkv_grads = [ex.send(B.qkv_src.at[:, q], B.qkv_terms.at[b], s, q) for q in ex.line()]
+    dh1_over = ex.sum_chips(dh1_pairs, B.dh1_src, B.dh1_pair, B.dh1_paired, B.dh1_chips, B.total)
+    da_passed = ex.gather_forward(da_copies, da_slot)
+    ffo = ex.sum_end(ffo_over, B.ffo_chips, B.ffo_total)
+    output[...] = jnp.where(held, B.residual[...] + ffo + bias_out, 0.0).astype(BF)
+    ex.arrived(da_passed)
+    terms = contract_rows(B.scaled[...].reshape(1024, 128), B.da_all[...].reshape(1024, 1024))
+    B.out_src[...] = terms.astype(BF).reshape(4, 32, 1024)
+    out_grads = [ex.send(B.out_src.at[q], B.out_terms.at[b], s, q) for q in ex.line()]
+
+    def line_sum(copies, mine, landed):
+        ex.arrived(copies)
+        total = mine
+        for k in (1, 2, 3):
+            total = total + landed[(b + k) % 4].astype(F32)
+        return total
+
+    grad_down[...] = line_sum(down_copies, B.down_src[b].astype(F32), B.down_terms)
+    B.up_own[...] = line_sum(up_grads, B.up_src[:, b].astype(F32), B.up_terms).astype(BF)
+    up_lanes = B.up_fin.at[:, columns(s * 512, 512)]
+    up_copies = [ex.send(B.up_own.at[p], up_lanes, p, b) for p in ex.plane()]
+    own_up = ex.local(B.up_own.at[s], up_lanes)
+
+    dh1 = ex.sum_end(dh1_over, B.dh1_chips, B.total)
+    normal_a, inverse_a = centred(x_in[...].astype(F32))
+    grad_input[...] = (B.dr[...] + norm_back(dh1, gain_a, normal_a, inverse_a)).astype(BF)
+    wide = jnp.concatenate(
+        [
+            column_sum(dh1 * normal_a),
+            sum_gain_b,
+            sum_gain_c,
+            column_sum(dh1),
+            sum_shift_b,
+            sum_shift_c,
+            jnp.zeros((1, 1024), F32),
+            sum_g,
+            jnp.zeros((1, 1024), F32),
+            sum_da,
+            jnp.zeros((6, 1024), F32),
+        ],
+        axis=0,
+    )
+    lane = lax.broadcasted_iota(jnp.int32, (1, 128), 1)
+    by_head = jnp.zeros((1, 128), F32)
+    for h in range(2):
+        found = jnp.sum(of_head(scale_sums / own_scale, h), axis=-1, keepdims=True)
+        by_head = jnp.where(lane == s * 2 + h, found, by_head)
+    place = lax.broadcasted_iota(jnp.int32, (16, 128), 0)
+    for p in range(8):
+        mine = jnp.where(s == p, 1.0, 0.0)
+        tile = wide[:, p * 128 : (p + 1) * 128]
+        tile = jnp.where(place == 6, sum_dq * mine, tile)
+        tile = jnp.where(place == 8, sum_dv * mine, tile)
+        B.close_src[p] = jnp.where(place == 10, by_head, tile)
+    for q in range(4):
+        part = [one[:, q * 128 : (q + 1) * 128] for one in ff_sums]
+        B.ff_src[q] = jnp.concatenate(part + [jnp.zeros((5, 128), F32)], axis=0)
+    close = [ex.send(B.close_src.at[p], B.close_all.at[me], p, q) for p, q in partners]
+    close_ff = [ex.send(B.ff_src.at[q], B.ff_all.at[b], s, q) for q in ex.line()]
+    own_close = [ex.local(B.close_src.at[s], B.close_all.at[me]), ex.local(B.ff_src.at[b], B.ff_all.at[b])]
+
+    B.qkv_own[...] = line_sum(qkv_grads, B.qkv_src[:, b].astype(F32), B.qkv_terms).astype(BF)
+    qkv_lanes = lambda t: B.qkv_fin.at[:, columns(t * 1024 + s * 128, 128)]
+    qkv_piece = lambda p, t: B.qkv_own.at[p, :, pl.ds(t * 128, 128)]
+    qkv_copies = [ex.send(qkv_piece(p, t), qkv_lanes(t), p, b) for p in ex.plane() for t in range(3)]
+    own_qkv = [ex.local(qkv_piece(s, t), qkv_lanes(t)) for t in range(3)]
+    grad_out[...] = line_sum(out_grads, B.out_src[b].astype(F32), B.out_terms)
+    ex.arrived(up_copies)
+    own_up.wait()
+    grad_up[...] = B.up_fin[...].astype(F32)
+    ex.arrived(close)
+    ex.arrived(close_ff)
+    for one in own_close:
+        one.wait()
+    total = B.close_all[0]
+    for i in range(1, 32):
+        total = total + B.close_all[i]
+    vec_out[...] = total
+    ff_out[...] = B.ff_all[0] + B.ff_all[1] + B.ff_all[2] + B.ff_all[3]
+    ex.arrived(qkv_copies)
+    for one in own_qkv:
+        one.wait()
+    grad_qkv[...] = B.qkv_fin[...].astype(F32)
+    ex.finish()
+
+
+def plane_shards(
+    inputs,
+    lengths,
+    w_qkv,
+    w_out,
+    w_up,
+    w_down,
+    norm_gains,
+    model_biases,
+    attn_biases,
+    ff_gain,
+    ff_biases,
+    head_scale,
+    cotangent,
+):
+    b = lax.axis_index("batch")
+    narrow = jnp.concatenate([norm_gains, model_biases, attn_biases]).astype(F32)
+    lanes = jnp.arange(128, dtype=jnp.int32) // 32
+    spread = jnp.where(lanes[None] == b, jnp.tile(narrow, (1, 4)), 0.0)
+    vectors = jnp.concatenate(
+        [spread, ff_gain[None].astype(F32), ff_biases.astype(F32), jnp.zeros((3, 128), F32)]
+    )
+    positions = lax.axis_index("seq") * 128 + jnp.arange(128, dtype=jnp.int32)
+    g_rows = jnp.where((positions < lengths[0])[:, None], cotangent[0], jnp.zeros((), BF))
+    near = pl.BlockSpec(memory_space=pltpu.VMEM)
+    outs = [
+        ((128, 1024), BF),
+        ((128, 1024), BF),
+        ((32, 3072), F32),
+        ((32, 1024), F32),
+        ((32, 4096), F32),
+        ((128, 1024), F32),
+        ((16, 128), F32),
+        ((8, 128), F32),
+    ]
+    found = pl.pallas_call(
+        block_kernel,
+        name="block",
+        out_shape=[jax.ShapeDtypeStruct(shape, dtype) for shape, dtype in outs],
+        in_specs=[pl.BlockSpec(memory_space=pltpu.SMEM)] + [near] * (INPUTS - 1),
+        out_specs=[near] * OUTPUTS,
+        scratch_shapes=[pltpu.VMEM(shape, dtype) for shape, dtype in BUFFERS.values()]
+        + [
+            pltpu.SemaphoreType.DMA((COPIES,)),
+            pltpu.SemaphoreType.DMA((COPIES,)),
+            pltpu.SemaphoreType.DMA((32,)),
+        ],
+        compiler_params=pltpu.CompilerParams(
+            collective_id=1, has_side_effects=True, vmem_limit_bytes=67043328
+        ),
+    )(
+        lengths.reshape(1, 1),
+        inputs[0],
+        g_rows,
+        w_qkv,
+        w_out,
+        w_up,
+        w_down,
+        vectors,
+        jnp.repeat(head_scale.astype(F32), HD).reshape(1, 1024),
+    )
+    output, grad_input, grad_qkv, grad_out, grad_up, grad_down, narrow, wide = found
+    narrow_own = lax.dynamic_slice_in_dim(narrow, b * 32, 32, 1)
+    return (
+        output[None],
+        grad_input[None],
+        grad_qkv,
+        grad_out,
+        grad_up,
+        grad_down,
+        narrow_own[0:3],
+        narrow_own[3:8],
+        narrow_own[8:10],
+        wide[0],
+        wide[1:3],
+        narrow[10, :H],
+    )
+
+
 def solution(mesh):
+    in_plane = mesh.shape["seq"] == 8 and mesh.shape["batch"] == 4
     return jax.shard_map(
-        shards,
+        plane_shards if in_plane else shards,
         mesh=mesh,
         in_specs=(
             P("batch", "seq", None),

time: 2470 us -> 204 us (0.08)
  the two profiles are of different devices: /device:TPU:0 before, /device:TPU:17 now
where the time goes in v1:
time: 204 us; the launch traced here: 203 us
  Pallas kernels  185 us (91%)
  local copies, waits for them, and re-layouts  14.5 us (7%)
  other arithmetic  2.45 us (1%)
    pallas_call x1, Pallas kernels, plane_shards(): pl.pallas_call(block_kernel, name='block', out_shape=[jax.ShapeDtypeStruc...  185 us
    unnamed x30, local copies, waits for them, and re-layouts  8.66 us

profile of v1, /device:TPU:17, one launch (start us, length us, event | category | flops | bytes accessed | tf_op | source)
XLA Modules:
  0.0 203.4 jit_solution(5436533865058005302)
XLA Ops:
  1.3 0.0 copy-start.10
  1.3 0.6 copy-done.10
  2.0 0.1 pad.3.clone
  2.1 0.6 copy-done.11
  2.6 0.0 copy-done.6
  2.7 0.6 copy-done.7
  3.3 0.0 copy-done.8
  3.3 0.6 copy-done.9
  4.0 0.1 broadcast_in_dim.44
  4.0 0.7 reshape_reshape.3.scale_in
  4.7 0.1 tile.10
  4.8 0.7 maximum_maximum_fusion.vec_in
  5.5 1.7 bitcast_select_fusion.g_in
  7.2 185.1 %block.1 = (bf16[128,1024]{1,0:T(8,128)(2,1)}, bf16[128,1024]{1,0:T(8,128)(2,1)}, f32[32,3072]{1,0:T(8,128)}, f32[32,1024]{1,0:T(8,128)}, f32[32,4096]{1,0:T(8,1...) custom-call(s32[1,1]{1,0:T(1,128)} %bitcast.14.length_in, bf16[128,1024]{1,0:T(8,128)(2,1)} %bitcast.16, ...), custom_call_target="tpu_custom_call" | custom-call | tf_op jit(solution)/shard_map/block/pallas_call | solution.py:897
  192.4 0.0 copy-start.5
  192.4 1.2 slice_bitcast_fusion.1
  193.6 1.2 slice.22
  194.8 0.0 copy-done.5
  194.8 0.5 slice_bitcast_fusion
  195.4 0.6 dynamic-slice.2
  196.0 0.6 constant_dynamic-slice_fusion
  196.6 0.7 dynamic-slice.1
  197.3 1.7 copy.32
  199.0 0.0 copy-done.3
  199.0 0.7 copy.33
  199.7 0.0 copy-done.2
  199.7 0.7 copy.34
  200.5 0.2 copy-done.4
  200.7 0.7 copy.35
  201.4 0.8 copy.36
  202.2 0.4 copy-done
  202.6 0.8 copy.37
  (19 shorter events, 0.1 us)
Async XLA Ops:
  1.3 0.7 copy-start.10
  2.0 0.7 copy-start.11
  2.0 0.7 copy-start.6
  2.6 0.7 copy-start.7
  2.6 0.7 copy-start.8
  3.3 0.7 copy-start.9
  192.4 2.5 %copy-start.5 = (f32[16,128]{1,0:T(8,128)S(1)}, f32[16,128]{1,0:T(8,128)}, u32[]{:S(2)}) copy-start(f32[16,128]{1,0:T(8,128)} %get-tuple-element.26) | copy-start | bytes 24580
  196.6 2.4 %copy-start.3 = (bf16[128,1024]{1,0:T(8,128)(2,1)S(1)}, bf16[128,1024]{1,0:T(8,128)(2,1)}, u32[]{:S(2)}) copy-start(bf16[128,1024]{1,0:T(8,128)(2,1)} %get-tuple-element.21) | copy-start | bytes 786436
  197.3 2.4 %copy-start.2 = (f32[32,3072]{1,0:T(8,128)S(1)}, f32[32,3072]{1,0:T(8,128)}, u32[]{:S(2)}) copy-start(f32[32,3072]{1,0:T(8,128)} %get-tuple-element.42) | copy-start | bytes 1179652
  199.7 1.0 copy-start.4
  199.7 1.7 copy-start.1
  201.4 1.2 copy-start

commit v2 on v1

--- a/solution.py
+++ b/solution.py
@@ -301,6 +301,7 @@
         self.count = 0
         self.locals = 0
         self.sent = []
+        self.sent_if = []
         self.s = lax.axis_index("seq")
         self.b = lax.axis_index("batch")
         self.chip = self.s // 2
@@ -322,6 +323,98 @@
         self.sent.append(copy)
         return copy
 
+    def describe(self, src, dst, seq, batch, sent_at, recv_at):
+        return pltpu.make_async_remote_copy(
+            src_ref=src,
+            dst_ref=dst,
+            send_sem=self.send_sems.at[sent_at],
+            recv_sem=self.recv_sems.at[recv_at],
+            device_id=(seq, batch),
+            device_id_type=pl.DeviceIdType.MESH,
+        )
+
+    def send_if(self, held, copy):
+        @pl.when(held)
+        def _():
+            copy.start()
+
+        self.sent_if.append((held, copy))
+
+    def line_start(self, src, slot):
+        first = self.count
+        self.count += 4
+        b = self.b
+        copies = [
+            self.describe(src, slot(b), self.s, (b + k) % 4, first + k - 1, first + k - 1) for k in (1, 2, 3)
+        ]
+        self.send_if(b != 3, copies[0])
+        self.send_if(b != 0, copies[2])
+        copies[1].start()
+        self.sent.append(copies[1])
+        return copies, slot, first
+
+    def line_relay(self, line):
+        copies, slot, first = line
+        b = self.b
+
+        @pl.when((b == 1) | (b == 2))
+        def _():
+            copies[1].wait_recv()
+
+        came = slot((b + 2) % 4)
+        self.send_if(b == 1, self.describe(came, came, self.s, 0, first + 3, first))
+        self.send_if(b == 2, self.describe(came, came, self.s, 3, first + 3, first + 2))
+
+    def line_arrived(self, line):
+        copies, _slot, _first = line
+        copies[0].wait_recv()
+        copies[2].wait_recv()
+
+        @pl.when((self.b == 0) | (self.b == 3))
+        def _():
+            copies[1].wait_recv()
+
+    def terms_start(self, view, landed, passing):
+        first = self.count
+        self.count += 4
+        b = self.b
+        at = lambda q, k: self.describe(view(q), landed.at[b], self.s, q, first + k - 1, first + k - 1)
+        up, over, down = at((b + 1) % 4, 1), at((b + 2) % 4, 2), at((b + 3) % 4, 3)
+        to_one = self.describe(view(3), passing, self.s, 1, first + 3, first + 3)
+        to_two = self.describe(view(0), passing, self.s, 2, first + 3, first + 3)
+        self.send_if(b == 0, to_one)
+        self.send_if(b == 3, to_two)
+        self.send_if((b == 0) | (b == 3), over)
+        self.send_if(b != 3, up)
+        self.send_if(b != 0, down)
+        return up, over, down, to_one, landed, passing, first
+
+    def terms_relay(self, terms, mine, joined):
+        up, over, down, to_one, landed, passing, first = terms
+        b = self.b
+        held = (b == 1) | (b == 2)
+
+        @pl.when(held)
+        def _():
+            to_one.wait_recv()
+            joined[...] = (mine((b + 2) % 4).astype(F32) + passing[...].astype(F32)).astype(BF)
+
+        self.send_if(
+            held, self.describe(joined, landed.at[b], self.s, (b + 2) % 4, first + 1, first + 1)
+        )
+
+    def terms_arrived(self, terms):
+        up, over, down = terms[:3]
+        over.wait_recv()
+
+        @pl.when(self.b != 0)
+        def _():
+            up.wait_recv()
+
+        @pl.when(self.b != 3)
+        def _():
+            down.wait_recv()
+
     def local(self, src, dst):
         at = self.locals
         self.locals += 1
@@ -336,6 +429,8 @@
     def finish(self):
         for copy in self.sent:
             copy.wait_send()
+        for held, copy in self.sent_if:
+            pl.when(held)(copy.wait_send)
 
     def peer(self, k):
         return ((self.chip + k) % 4) * 2 + self.core
@@ -432,7 +527,9 @@
     out_w=((8, 4, 32, 1024), BF),
     up_w=((8, 4, 32, 512), BF),
     down_w=((4, 128, 1024), BF),
+    vec_src=((16, 128), F32),
     vec_all=((32, 16, 128), F32),
+    scale_row=((8, 1024), F32),
     rows=((16, 1024), F32),
     ff_rows=((8, 512), F32),
     h1=((1024, 1024), BF),
@@ -453,7 +550,6 @@
     stats_all=((8, 8, 8, 128), F32),
     u2=((1024, 512), BF),
     dz=((1024, 512), BF),
-    dh2_src=((8, 128, 1024), BF),
     dh2_pair=((4, 128, 1024), BF),
     dh2_paired=((3, 128, 1024), BF),
     dh2_chips=((3, 128, 1024), BF),
@@ -481,6 +577,12 @@
     down_terms=((4, 128, 1024), BF),
     qkv_src=((8, 4, 32, 384), BF),
     qkv_terms=((4, 8, 32, 384), BF),
+    up_passing=((8, 32, 512), BF),
+    up_joined=((8, 32, 512), BF),
+    down_passing=((128, 1024), BF),
+    down_joined=((128, 1024), BF),
+    qkv_passing=((8, 32, 384), BF),
+    qkv_joined=((8, 32, 384), BF),
     out_src=((4, 32, 1024), BF),
     out_terms=((4, 32, 1024), BF),
     up_own=((8, 32, 512), BF),
@@ -493,17 +595,63 @@
     ff_all=((4, 8, 128), F32),
 )
 COPIES = 240
-INPUTS = 9
+INPUTS = 13
 OUTPUTS = 8
 
 
-def block_kernel(length_in, x_in, g_in, qkv_in, out_in, up_in, down_in, vec_in, scale_in, *refs):
+def block_kernel(
+    length_in,
+    x_in,
+    g_in,
+    qkv_in,
+    out_in,
+    up_in,
+    down_in,
+    gains_in,
+    biases_in,
+    attn_in,
+    ff_gain_in,
+    ff_bias_in,
+    scale_in,
+    *refs,
+):
     output, grad_input, grad_qkv, grad_out, grad_up, grad_down, vec_out, ff_out = refs[:OUTPUTS]
     B = type("Buffers", (), dict(zip(BUFFERS, refs[OUTPUTS : OUTPUTS + len(BUFFERS)])))
     ex = Exchange(*refs[OUTPUTS + len(BUFFERS) :])
     s, b = ex.s, ex.b
     me = s * 4 + b
     valid_rows = length_in[0, 0]
+
+    lane = lax.broadcasted_iota(jnp.int32, (1, 128), 1)
+
+    def spread(part):
+        values = part[...].astype(F32)
+        return jnp.where(lane // 32 == b, jnp.concatenate([values] * 4, axis=1), 0.0)
+
+    B.vec_src[0:3, :] = spread(gains_in)
+    B.vec_src[3:8, :] = spread(biases_in)
+    B.vec_src[8:10, :] = spread(attn_in)
+    B.vec_src[10:11, :] = ff_gain_in[...].astype(F32)
+    B.vec_src[11:13, :] = ff_bias_in[...].astype(F32)
+    B.vec_src[13:16, :] = jnp.zeros((3, 128), F32)
+    held = s * 128 + lax.broadcasted_iota(jnp.int32, (128, 1), 0) < valid_rows
+    B.g_all[s] = jnp.where(held, g_in[...].astype(F32), 0.0).astype(BF)
+    by_head = lax.broadcasted_iota(jnp.int32, (8, 1024), 1) // HD
+    head_scales = scale_in[...].astype(F32)
+    scale_row = jnp.zeros((8, 1024), F32)
+    for h in range(H):
+        scale_row = jnp.where(by_head == h, head_scales[0:1, h : h + 1], scale_row)
+    B.scale_row[...] = scale_row
+
+    for landed in (B.up_terms, B.down_terms, B.qkv_terms):
+
+        @pl.when(b == 3)
+        def _():
+            landed[0] = jnp.zeros(landed.shape[1:], BF)
+
+        @pl.when(b == 0)
+        def _():
+            landed[3] = jnp.zeros(landed.shape[1:], BF)
 
     barrier = pltpu.get_barrier_semaphore()
     partners = [((s + j // 4) % 8, (b + j % 4) % 4) for j in range(1, 32)]
@@ -519,26 +667,26 @@
     own_rest = [
         ex.local(out_in, B.out_w.at[s, b]),
         ex.local(x_in, B.x_all.at[s]),
-        ex.local(g_in, B.g_all.at[s]),
         ex.local(down_in, B.down_w.at[b]),
-        ex.local(vec_in, B.vec_all.at[me]),
+        ex.local(B.vec_src, B.vec_all.at[me]),
     ]
     x_slot = lambda i: B.x_all.at[i]
     g_slot = lambda i: B.g_all.at[i]
     x_copies = ex.gather_start(x_in, x_slot)
-    vec_copies = [ex.send(vec_in, B.vec_all.at[me], p, q) for p, q in partners]
+    vec_copies = [ex.send(B.vec_src, B.vec_all.at[me], p, q) for p, q in partners]
     up_copies = [ex.send(up_in.at[:, columns(p * 512, 512)], B.up_w.at[s, b], p, b) for p in ex.plane()]
     ex.arrived(qkv_copies)
     for one in own:
         one.wait()
-    qkv_line = [ex.send(B.qkv_w.at[:, b], B.qkv_w.at[:, b], s, q) for q in ex.line()]
-    out_line = [ex.send(out_in, B.out_w.at[s, b], s, q) for q in ex.line()]
-    down_line = [ex.send(down_in, B.down_w.at[b], s, q) for q in ex.line()]
+    qkv_line = ex.line_start(B.qkv_w.at[:, b], lambda i: B.qkv_w.at[:, i])
     x_passed = ex.gather_forward(x_copies, x_slot)
-    g_copies = ex.gather_start(g_in, g_slot)
     ex.arrived(up_copies)
     own_up.wait()
-    up_line = [ex.send(B.up_w.at[:, b], B.up_w.at[:, b], s, q) for q in ex.line()]
+    ex.line_relay(qkv_line)
+    out_line = ex.line_start(out_in, lambda i: B.out_w.at[s, i])
+    down_line = ex.line_start(down_in, lambda i: B.down_w.at[i])
+    up_line = ex.line_start(B.up_w.at[:, b], lambda i: B.up_w.at[:, i])
+    g_copies = ex.gather_start(B.g_all.at[s], g_slot)
     ex.arrived(vec_copies)
     for one in own_rest:
         one.wait()
@@ -555,7 +703,7 @@
     own_columns = columns(s * 128, 128)
     query_bias = B.rows[6:7, own_columns]
     value_bias = B.rows[8:9, own_columns]
-    own_scale = scale_in[0:1, own_columns]
+    own_scale = B.scale_row[0:1, own_columns]
 
     ex.arrived(x_passed)
 
@@ -564,7 +712,7 @@
         normal, _unused = centred(B.x_all[t].astype(F32))
         B.h1[pl.ds(t * 128, 128), :] = (normal * gain_a + bias_a).astype(BF)
 
-    ex.arrived(qkv_line)
+    ex.line_arrived(qkv_line)
     offsets = jnp.concatenate([query_bias, jnp.zeros_like(query_bias), value_bias], axis=1)
 
     @pl.loop(0, 4)
@@ -572,7 +720,8 @@
         at = pl.ds(t * 256, 256)
         B.qkv[at, :] = (matmul(B.h1[at, :], B.qkv_w[...].reshape(1024, 384)) + offsets).astype(BF)
 
-    ex.arrived(out_line)
+    ex.line_relay(out_line)
+    ex.line_arrived(out_line)
     out_slot = lambda i: B.out_w.at[i]
     out_copies = ex.gather_start(B.out_w.at[s], out_slot)
     g_passed = ex.gather_forward(g_copies, g_slot)
@@ -611,6 +760,7 @@
     own_heads = ex.local(B.scaled.at[s], local_lanes)
     out_passed = ex.gather_forward(out_copies, out_slot)
     ex.arrived(out_passed)
+    ex.line_relay(down_line)
     ex.arrived(heads)
     own_heads.wait()
 
@@ -626,14 +776,15 @@
     h2_copies = ex.gather_start(B.h2_all.at[s], h2_slot)
 
     ex.arrived(g_passed)
-    ex.arrived(down_line)
+    ex.line_relay(up_line)
+    ex.line_arrived(down_line)
 
     @pl.loop(0, 8)
     def _(t):
         B.du2[pl.ds(t * 128, 128), :] = times_transposed(B.g_all[t], B.down_w[...].reshape(512, 1024))
 
     h2_passed = ex.gather_forward(h2_copies, h2_slot)
-    ex.arrived(up_line)
+    ex.line_arrived(up_line)
     ex.arrived(h2_passed)
 
     @pl.loop(0, 8)
@@ -653,6 +804,10 @@
     own_stats = ex.local(B.stats, B.stats_all.at[s])
     ex.arrived(stats_copies)
     own_stats.wait()
+
+    for copy in x_passed[1:]:
+        copy.wait_send()
+        ex.sent = [one for one in ex.sent if one is not copy]
 
     def finish_hidden(t, sums):
         at = pl.ds(t * 128, 128)
@@ -673,7 +828,7 @@
         du2 = B.du2[at, :]
         dz = (inverse * (du2 * ffn_gain - average - normal * along) * B.slope[at, :]).astype(BF)
         B.dz[at, :] = dz
-        B.dh2_src[t] = times_transposed(dz, B.up_w[...].reshape(1024, 512)).astype(BF)
+        B.x_all[t] = times_transposed(dz, B.up_w[...].reshape(1024, 512)).astype(BF)
         return (
             sums[0] + column_sum(du2 * normal),
             sums[1] + column_sum(dz.astype(F32)),
@@ -682,13 +837,13 @@
 
     nothing = jnp.zeros((1, 512), F32)
     ff_sums = lax.fori_loop(0, 8, finish_hidden, (nothing, nothing, nothing))
-    dh2_pairs = ex.sum_pair(B.dh2_src, B.dh2_pair)
+    dh2_pairs = ex.sum_pair(B.x_all, B.dh2_pair)
 
     @pl.loop(0, 8)
     def _(t):
         B.ffo_src[t] = matmul(B.u2[pl.ds(t * 128, 128), :], B.down_w[...].reshape(512, 1024)).astype(BF)
 
-    dh2_over = ex.sum_chips(dh2_pairs, B.dh2_src, B.dh2_pair, B.dh2_paired, B.dh2_chips, B.total)
+    dh2_over = ex.sum_chips(dh2_pairs, B.x_all, B.dh2_pair, B.dh2_paired, B.dh2_chips, B.total)
     ffo_pairs = ex.sum_pair(B.ffo_src, B.ffo_pair)
 
     @pl.loop(0, 4)
@@ -696,29 +851,30 @@
         terms = contract_rows(B.u2[:, columns(q * 128, 128)], B.g_all[...].reshape(1024, 1024))
         B.down_src[q] = terms.astype(BF)
 
-    down_copies = [ex.send(B.down_src.at[q], B.down_terms.at[b], s, q) for q in ex.line()]
+    down_grads = ex.terms_start(lambda q: B.down_src.at[q], B.down_terms, B.down_passing)
 
     @pl.loop(0, 8)
     def _(c):
         rows = B.h2_all[:, :, columns(c * 128, 128)].reshape(1024, 128)
         B.up_src[c] = contract_rows(rows, B.dz[...]).astype(BF).reshape(4, 32, 512)
 
-    up_grads = [ex.send(B.up_src.at[:, q], B.up_terms.at[b], s, q) for q in ex.line()]
+    up_grads = ex.terms_start(lambda q: B.up_src.at[:, q], B.up_terms, B.up_passing)
 
     dh2 = ex.sum_end(dh2_over, B.dh2_chips, B.total)
     sum_gain_c = column_sum(dh2 * B.normal_c[...])
     sum_shift_c = column_sum(dh2)
-    held = s * 128 + lax.broadcasted_iota(jnp.int32, (128, 1), 0) < valid_rows
-    g_local = g_in[...].astype(F32)
+    g_local = B.g_all[s].astype(F32)
     dr = g_local + norm_back(dh2, gain_c, B.normal_c[...], inverse_c)
     B.dr[...] = dr
     da = norm_back(dr, gain_b, B.normal_b[...], inverse_b).astype(BF)
     B.da_all[s] = da
-    B.do_local[...] = (times_transposed(da, B.out_w[...].reshape(1024, 1024)) * scale_in[0:1, :]).astype(BF)
+    B.do_local[...] = (times_transposed(da, B.out_w[...].reshape(1024, 1024)) * B.scale_row[0:1, :]).astype(BF)
     do_copies = [ex.send(B.do_local.at[:, columns(p * 128, 128)], B.do_all.at[s], p, b) for p in ex.plane()]
     own_do = ex.local(B.do_local.at[:, own_columns], B.do_all.at[s])
     da_slot = lambda i: B.da_all.at[i]
     da_copies = ex.gather_start(B.da_all.at[s], da_slot)
+    ex.terms_relay(down_grads, lambda q: B.down_src[q], B.down_joined)
+    ex.terms_relay(up_grads, lambda q: B.up_src[:, q], B.up_joined)
     ffo_over = ex.sum_chips(ffo_pairs, B.ffo_src, B.ffo_pair, B.ffo_paired, B.ffo_chips, B.ffo_total)
     sum_gain_b = column_sum(dr * B.normal_b[...])
     sum_shift_b = column_sum(dr)
@@ -773,8 +929,9 @@
         terms = contract_rows(B.h1[:, columns(c * 128, 128)], B.dqkv[...])
         B.qkv_src[c] = terms.astype(BF).reshape(4, 32, 384)
 
-    qkv_grads = [ex.send(B.qkv_src.at[:, q], B.qkv_terms.at[b], s, q) for q in ex.line()]
+    qkv_grads = ex.terms_start(lambda q: B.qkv_src.at[:, q], B.qkv_terms, B.qkv_passing)
     dh1_over = ex.sum_chips(dh1_pairs, B.dh1_src, B.dh1_pair, B.dh1_paired, B.dh1_chips, B.total)
+    ex.terms_relay(qkv_grads, lambda q: B.qkv_src[:, q], B.qkv_joined)
     da_passed = ex.gather_forward(da_copies, da_slot)
     ffo = ex.sum_end(ffo_over, B.ffo_chips, B.ffo_total)
     output[...] = jnp.where(held, B.residual[...] + ffo + bias_out, 0.0).astype(BF)
@@ -783,15 +940,16 @@
     B.out_src[...] = terms.astype(BF).reshape(4, 32, 1024)
     out_grads = [ex.send(B.out_src.at[q], B.out_terms.at[b], s, q) for q in ex.line()]
 
-    def line_sum(copies, mine, landed):
-        ex.arrived(copies)
+    def line_sum(mine, landed):
         total = mine
         for k in (1, 2, 3):
             total = total + landed[(b + k) % 4].astype(F32)
         return total
 
-    grad_down[...] = line_sum(down_copies, B.down_src[b].astype(F32), B.down_terms)
-    B.up_own[...] = line_sum(up_grads, B.up_src[:, b].astype(F32), B.up_terms).astype(BF)
+    ex.terms_arrived(down_grads)
+    grad_down[...] = line_sum(B.down_src[b].astype(F32), B.down_terms)
+    ex.terms_arrived(up_grads)
+    B.up_own[...] = line_sum(B.up_src[:, b].astype(F32), B.up_terms).astype(BF)
     up_lanes = B.up_fin.at[:, columns(s * 512, 512)]
     up_copies = [ex.send(B.up_own.at[p], up_lanes, p, b) for p in ex.plane()]
     own_up = ex.local(B.up_own.at[s], up_lanes)
@@ -815,7 +973,6 @@
         ],
         axis=0,
     )
-    lane = lax.broadcasted_iota(jnp.int32, (1, 128), 1)
     by_head = jnp.zeros((1, 128), F32)
     for h in range(2):
         found = jnp.sum(of_head(scale_sums / own_scale, h), axis=-1, keepdims=True)
@@ -834,12 +991,14 @@
     close_ff = [ex.send(B.ff_src.at[q], B.ff_all.at[b], s, q) for q in ex.line()]
     own_close = [ex.local(B.close_src.at[s], B.close_all.at[me]), ex.local(B.ff_src.at[b], B.ff_all.at[b])]
 
-    B.qkv_own[...] = line_sum(qkv_grads, B.qkv_src[:, b].astype(F32), B.qkv_terms).astype(BF)
+    ex.terms_arrived(qkv_grads)
+    B.qkv_own[...] = line_sum(B.qkv_src[:, b].astype(F32), B.qkv_terms).astype(BF)
     qkv_lanes = lambda t: B.qkv_fin.at[:, columns(t * 1024 + s * 128, 128)]
     qkv_piece = lambda p, t: B.qkv_own.at[p, :, pl.ds(t * 128, 128)]
     qkv_copies = [ex.send(qkv_piece(p, t), qkv_lanes(t), p, b) for p in ex.plane() for t in range(3)]
     own_qkv = [ex.local(qkv_piece(s, t), qkv_lanes(t)) for t in range(3)]
-    grad_out[...] = line_sum(out_grads, B.out_src[b].astype(F32), B.out_terms)
+    ex.arrived(out_grads)
+    grad_out[...] = line_sum(B.out_src[b].astype(F32), B.out_terms)
     ex.arrived(up_copies)
     own_up.wait()
     grad_up[...] = B.up_fin[...].astype(F32)
@@ -875,14 +1034,6 @@
     cotangent,
 ):
     b = lax.axis_index("batch")
-    narrow = jnp.concatenate([norm_gains, model_biases, attn_biases]).astype(F32)
-    lanes = jnp.arange(128, dtype=jnp.int32) // 32
-    spread = jnp.where(lanes[None] == b, jnp.tile(narrow, (1, 4)), 0.0)
-    vectors = jnp.concatenate(
-        [spread, ff_gain[None].astype(F32), ff_biases.astype(F32), jnp.zeros((3, 128), F32)]
-    )
-    positions = lax.axis_index("seq") * 128 + jnp.arange(128, dtype=jnp.int32)
-    g_rows = jnp.where((positions < lengths[0])[:, None], cotangent[0], jnp.zeros((), BF))
     near = pl.BlockSpec(memory_space=pltpu.VMEM)
     outs = [
         ((128, 1024), BF),
@@ -912,13 +1063,17 @@
     )(
         lengths.reshape(1, 1),
         inputs[0],
-        g_rows,
+        cotangent[0],
         w_qkv,
         w_out,
         w_up,
         w_down,
-        vectors,
-        jnp.repeat(head_scale.astype(F32), HD).reshape(1, 1024),
+        norm_gains,
+        model_biases,
+        attn_biases,
+        ff_gain.reshape(1, 128),
+        ff_biases,
+        head_scale.reshape(1, H),
     )
     output, grad_input, grad_qkv, grad_out, grad_up, grad_down, narrow, wide = found
     narrow_own = lax.dynamic_slice_in_dim(narrow, b * 32, 32, 1)

time: 204 us -> 191 us (0.936)
  the two profiles are of different devices: /device:TPU:17 before, /device:TPU:0 now
where the time goes in v2:
time: 191 us
  Pallas kernels  178 us (93%)
  local copies, waits for them, and re-layouts  11 us (6%)
    pallas_call x1, Pallas kernels, plane_shards(): pl.pallas_call(block_kernel, name='block', out_shape=[jax.ShapeDtypeStruc...  178 us
    unnamed x18, local copies, waits for them, and re-layouts  6.11 us

profile of v2, /device:TPU:0, one launch (start us, length us, event | category | flops | bytes accessed | tf_op | source)
XLA Modules:
  0.0 190.8 jit_solution(15270107830961313610)
XLA Ops:
  1.3 178.4 %block.1 = (bf16[128,1024]{1,0:T(8,128)(2,1)}, bf16[128,1024]{1,0:T(8,128)(2,1)}, f32[32,3072]{1,0:T(8,128)}, f32[32,1024]{1,0:T(8,128)}, f32[32,4096]{1,0:T(8,1...) custom-call(s32[1,1]{1,0:T(1,128)} %bitcast.11.length_in, bf16[128,1024]{1,0:T(8,128)(2,1)} %bitcast.14, ...), custom_call_target="tpu_custom_call" | custom-call | tf_op jit(solution)/shard_map/block/pallas_call | solution.py:1048
  179.7 0.0 copy-start.5
  179.8 1.2 slice_bitcast_fusion.1
  181.0 1.2 slice.22
  182.2 0.0 copy-done.5
  182.2 0.5 slice_bitcast_fusion
  182.7 0.6 dynamic-slice.2
  183.3 0.6 constant_dynamic-slice_fusion
  184.0 0.0 copy-start.3
  184.0 0.7 dynamic-slice.1
  184.7 0.0 copy-start.2
  184.7 1.7 copy.32
  186.4 0.0 copy-done.3
  186.4 0.7 copy.33
  187.1 0.0 copy-done.2
  187.1 0.0 copy-start.4
  187.1 0.0 copy-start.1
  187.1 0.7 copy.34
  187.8 0.2 copy-done.4
  188.1 0.7 copy.35
  188.7 0.0 copy-done.1
  188.8 0.0 copy-start
  188.8 0.8 copy.36
  189.5 0.4 copy-done
  190.0 0.8 copy.37
Async XLA Ops:
  179.7 2.5 %copy-start.5 = (f32[16,128]{1,0:T(8,128)S(1)}, f32[16,128]{1,0:T(8,128)}, u32[]{:S(2)}) copy-start(f32[16,128]{1,0:T(8,128)} %get-tuple-element.26) | copy-start | bytes 24580
  184.0 2.4 %copy-start.3 = (bf16[128,1024]{1,0:T(8,128)(2,1)S(1)}, bf16[128,1024]{1,0:T(8,128)(2,1)}, u32[]{:S(2)}) copy-start(bf16[128,1024]{1,0:T(8,128)(2,1)} %get-tuple-element.21) | copy-start | bytes 786436
  184.7 2.4 %copy-start.2 = (f32[32,3072]{1,0:T(8,128)S(1)}, f32[32,3072]{1,0:T(8,128)}, u32[]{:S(2)}) copy-start(f32[32,3072]{1,0:T(8,128)} %get-tuple-element.42) | copy-start | bytes 1179652
  187.1 1.0 copy-start.4
  187.1 1.7 copy-start.1
  188.8 1.2 copy-start

commit v3 on v2

--- a/solution.py
+++ b/solution.py
@@ -347,11 +347,14 @@
         copies = [
             self.describe(src, slot(b), self.s, (b + k) % 4, first + k - 1, first + k - 1) for k in (1, 2, 3)
         ]
-        self.send_if(b != 3, copies[0])
-        self.send_if(b != 0, copies[2])
         copies[1].start()
         self.sent.append(copies[1])
         return copies, slot, first
+
+    def line_near(self, line):
+        copies = line[0]
+        self.send_if(self.b != 3, copies[0])
+        self.send_if(self.b != 0, copies[2])
 
     def line_relay(self, line):
         copies, slot, first = line
@@ -437,6 +440,12 @@
 
     def source(self, k):
         return ((self.chip + 4 - k) % 4) * 2 + self.core
+
+    def chip_source(self, k):
+        return (self.chip + 4 - k) % 4
+
+    def tile(self, j):
+        return (self.chip + j + 1) % 4 * 2 + jnp.where(j < 4, 1 - self.core, self.core)
 
     def plane(self):
         return [(self.s + j) % 8 for j in range(1, 8)]
@@ -586,9 +595,7 @@
     out_src=((4, 32, 1024), BF),
     out_terms=((4, 32, 1024), BF),
     up_own=((8, 32, 512), BF),
-    up_fin=((32, 4096), BF),
     qkv_own=((8, 32, 384), BF),
-    qkv_fin=((32, 3072), BF),
     close_src=((8, 16, 128), F32),
     close_all=((32, 16, 128), F32),
     ff_src=((4, 8, 128), F32),
@@ -615,7 +622,7 @@
     scale_in,
     *refs,
 ):
-    output, grad_input, grad_qkv, grad_out, grad_up, grad_down, vec_out, ff_out = refs[:OUTPUTS]
+    output, grad_input, qkv_fin, grad_out, up_fin, grad_down, vec_out, ff_out = refs[:OUTPUTS]
     B = type("Buffers", (), dict(zip(BUFFERS, refs[OUTPUTS : OUTPUTS + len(BUFFERS)])))
     ex = Exchange(*refs[OUTPUTS + len(BUFFERS) :])
     s, b = ex.s, ex.b
@@ -662,6 +669,8 @@
     qkv_part = lambda p, t: qkv_in.at[:, columns(t * 1024 + p * 128, 128)]
     qkv_slot = lambda t: B.qkv_w.at[s, b, :, pl.ds(t * 128, 128)]
     qkv_copies = [ex.send(qkv_part(p, t), qkv_slot(t), p, b) for p in ex.plane() for t in range(3)]
+    out_line = ex.line_start(out_in, lambda i: B.out_w.at[s, i])
+    ex.line_near(out_line)
     own = [ex.local(qkv_part(s, t), qkv_slot(t)) for t in range(3)]
     own_up = ex.local(up_in.at[:, columns(s * 512, 512)], B.up_w.at[s, b])
     own_rest = [
@@ -679,13 +688,16 @@
     for one in own:
         one.wait()
     qkv_line = ex.line_start(B.qkv_w.at[:, b], lambda i: B.qkv_w.at[:, i])
+    ex.line_near(qkv_line)
+    ex.line_relay(out_line)
     x_passed = ex.gather_forward(x_copies, x_slot)
     ex.arrived(up_copies)
     own_up.wait()
     ex.line_relay(qkv_line)
-    out_line = ex.line_start(out_in, lambda i: B.out_w.at[s, i])
     down_line = ex.line_start(down_in, lambda i: B.down_w.at[i])
     up_line = ex.line_start(B.up_w.at[:, b], lambda i: B.up_w.at[:, i])
+    ex.line_near(down_line)
+    ex.line_near(up_line)
     g_copies = ex.gather_start(B.g_all.at[s], g_slot)
     ex.arrived(vec_copies)
     for one in own_rest:
@@ -720,7 +732,6 @@
         at = pl.ds(t * 256, 256)
         B.qkv[at, :] = (matmul(B.h1[at, :], B.qkv_w[...].reshape(1024, 384)) + offsets).astype(BF)
 
-    ex.line_relay(out_line)
     ex.line_arrived(out_line)
     out_slot = lambda i: B.out_w.at[i]
     out_copies = ex.gather_start(B.out_w.at[s], out_slot)
@@ -733,6 +744,9 @@
         return jnp.where(half_of == h, rows, jnp.zeros_like(rows))
 
     for size in (512, 1024):
+        if size == 1024:
+            ex.line_relay(down_line)
+            ex.line_relay(up_line)
         for h in range(2):
 
             @pl.loop(size // 128 - 4, size // 128)
@@ -760,7 +774,6 @@
     own_heads = ex.local(B.scaled.at[s], local_lanes)
     out_passed = ex.gather_forward(out_copies, out_slot)
     ex.arrived(out_passed)
-    ex.line_relay(down_line)
     ex.arrived(heads)
     own_heads.wait()
 
@@ -776,22 +789,15 @@
     h2_copies = ex.gather_start(B.h2_all.at[s], h2_slot)
 
     ex.arrived(g_passed)
-    ex.line_relay(up_line)
     ex.line_arrived(down_line)
-
-    @pl.loop(0, 8)
-    def _(t):
+    ex.line_arrived(up_line)
+
+    def upstream(t):
         B.du2[pl.ds(t * 128, 128), :] = times_transposed(B.g_all[t], B.down_w[...].reshape(512, 1024))
 
-    h2_passed = ex.gather_forward(h2_copies, h2_slot)
-    ex.line_arrived(up_line)
-    ex.arrived(h2_passed)
-
-    @pl.loop(0, 8)
-    def _(t):
+    def hidden_tile(t):
         at = pl.ds(t * 128, 128)
-        hidden = matmul(B.h2_all[t], B.up_w[...].reshape(1024, 512)) + ffn_bias
-        active, slope = gelu_parts(hidden)
+        active, slope = gelu_parts(matmul(B.h2_all[t], B.up_w[...].reshape(1024, 512)) + ffn_bias)
         B.active[at, :] = active
         B.slope[at, :] = slope
         dgain = B.du2[at, :] * ffn_gain
@@ -800,6 +806,20 @@
         add = lambda rows: jnp.sum(rows, axis=-1, keepdims=True)
         B.stats[t] = pack_columns([mean, add(off * off), add(dgain), add(dgain * off)])
 
+    pl.loop(0, 8)(upstream)
+    hidden_tile(s)
+    h2_copies[3].wait_recv()
+    hidden_tile(ex.sibling)
+    h2_passed = []
+    for k in (1, 3, 2):
+        h2_copies[k - 1].wait_recv()
+        came = h2_slot(ex.source(k))
+        h2_passed.append(ex.send(came, came, ex.sibling, b))
+        hidden_tile(ex.source(k))
+    for at, k in enumerate((1, 3, 2)):
+        h2_passed[at].wait_recv()
+        hidden_tile(ex.chip_source(k) * 2 + 1 - ex.core)
+
     stats_copies = [ex.send(B.stats, B.stats_all.at[s], p, b) for p in ex.plane()]
     own_stats = ex.local(B.stats, B.stats_all.at[s])
     ex.arrived(stats_copies)
@@ -809,7 +829,8 @@
         copy.wait_send()
         ex.sent = [one for one in ex.sent if one is not copy]
 
-    def finish_hidden(t, sums):
+    def finish_hidden(j, sums):
+        t = ex.tile(j)
         at = pl.ds(t * 128, 128)
         means = [B.stats_all[i, t, 0:1, :] for i in range(8)]
         squares = [B.stats_all[i, t, 1:2, :] for i in range(8)]
@@ -836,15 +857,10 @@
         )
 
     nothing = jnp.zeros((1, 512), F32)
-    ff_sums = lax.fori_loop(0, 8, finish_hidden, (nothing, nothing, nothing))
+    ff_sums = lax.fori_loop(0, 4, finish_hidden, (nothing, nothing, nothing))
     dh2_pairs = ex.sum_pair(B.x_all, B.dh2_pair)
-
-    @pl.loop(0, 8)
-    def _(t):
-        B.ffo_src[t] = matmul(B.u2[pl.ds(t * 128, 128), :], B.down_w[...].reshape(512, 1024)).astype(BF)
-
+    ff_sums = lax.fori_loop(4, 8, finish_hidden, ff_sums)
     dh2_over = ex.sum_chips(dh2_pairs, B.x_all, B.dh2_pair, B.dh2_paired, B.dh2_chips, B.total)
-    ffo_pairs = ex.sum_pair(B.ffo_src, B.ffo_pair)
 
     @pl.loop(0, 4)
     def _(q):
@@ -859,6 +875,12 @@
         B.up_src[c] = contract_rows(rows, B.dz[...]).astype(BF).reshape(4, 32, 512)
 
     up_grads = ex.terms_start(lambda q: B.up_src.at[:, q], B.up_terms, B.up_passing)
+
+    @pl.loop(0, 8)
+    def _(t):
+        B.ffo_src[t] = matmul(B.u2[pl.ds(t * 128, 128), :], B.down_w[...].reshape(512, 1024)).astype(BF)
+
+    ffo_pairs = ex.sum_pair(B.ffo_src, B.ffo_pair)
 
     dh2 = ex.sum_end(dh2_over, B.dh2_chips, B.total)
     sum_gain_c = column_sum(dh2 * B.normal_c[...])
@@ -917,11 +939,16 @@
         B.dqkv[at, 0:128] = dq
         B.dqkv[at, 128:256] = dk
         B.dqkv[at, 256:384] = dv
-        B.dh1_src[t] = times_transposed(B.dqkv[at, :], B.qkv_w[...].reshape(1024, 384)).astype(BF)
         return (sums[0] + column_sum(dq.astype(F32)), sums[1] + column_sum(dv.astype(F32)))
+
+    def dh1_tile(j):
+        t = ex.tile(j)
+        rows = B.dqkv[pl.ds(t * 128, 128), :]
+        B.dh1_src[t] = times_transposed(rows, B.qkv_w[...].reshape(1024, 384)).astype(BF)
 
     blank = jnp.zeros((1, 128), F32)
     sum_dq, sum_dv = lax.fori_loop(0, 8, join, (blank, blank))
+    pl.loop(0, 4)(dh1_tile)
     dh1_pairs = ex.sum_pair(B.dh1_src, B.dh1_pair)
 
     @pl.loop(0, 8)
@@ -930,6 +957,7 @@
         B.qkv_src[c] = terms.astype(BF).reshape(4, 32, 384)
 
     qkv_grads = ex.terms_start(lambda q: B.qkv_src.at[:, q], B.qkv_terms, B.qkv_passing)
+    pl.loop(4, 8)(dh1_tile)
     dh1_over = ex.sum_chips(dh1_pairs, B.dh1_src, B.dh1_pair, B.dh1_paired, B.dh1_chips, B.total)
     ex.terms_relay(qkv_grads, lambda q: B.qkv_src[:, q], B.qkv_joined)
     da_passed = ex.gather_forward(da_copies, da_slot)
@@ -950,7 +978,7 @@
     grad_down[...] = line_sum(B.down_src[b].astype(F32), B.down_terms)
     ex.terms_arrived(up_grads)
     B.up_own[...] = line_sum(B.up_src[:, b].astype(F32), B.up_terms).astype(BF)
-    up_lanes = B.up_fin.at[:, columns(s * 512, 512)]
+    up_lanes = up_fin.at[:, columns(s * 512, 512)]
     up_copies = [ex.send(B.up_own.at[p], up_lanes, p, b) for p in ex.plane()]
     own_up = ex.local(B.up_own.at[s], up_lanes)
 
@@ -993,7 +1021,7 @@
 
     ex.terms_arrived(qkv_grads)
     B.qkv_own[...] = line_sum(B.qkv_src[:, b].astype(F32), B.qkv_terms).astype(BF)
-    qkv_lanes = lambda t: B.qkv_fin.at[:, columns(t * 1024 + s * 128, 128)]
+    qkv_lanes = lambda t: qkv_fin.at[:, columns(t * 1024 + s * 128, 128)]
     qkv_piece = lambda p, t: B.qkv_own.at[p, :, pl.ds(t * 128, 128)]
     qkv_copies = [ex.send(qkv_piece(p, t), qkv_lanes(t), p, b) for p in ex.plane() for t in range(3)]
     own_qkv = [ex.local(qkv_piece(s, t), qkv_lanes(t)) for t in range(3)]
@@ -1001,7 +1029,6 @@
     grad_out[...] = line_sum(B.out_src[b].astype(F32), B.out_terms)
     ex.arrived(up_copies)
     own_up.wait()
-    grad_up[...] = B.up_fin[...].astype(F32)
     ex.arrived(close)
     ex.arrived(close_ff)
     for one in own_close:
@@ -1014,8 +1041,27 @@
     ex.arrived(qkv_copies)
     for one in own_qkv:
         one.wait()
-    grad_qkv[...] = B.qkv_fin[...].astype(F32)
     ex.finish()
+
+
+def finish_kernel(output, grad_input, qkv, out, up, down, narrow, wide, *outs):
+    b = lax.axis_index("batch")
+    outs[0][0] = output[...]
+    outs[1][0] = grad_input[...]
+    outs[2][...] = qkv[...].astype(F32)
+    outs[3][...] = out[...]
+    outs[4][...] = up[...].astype(F32)
+    outs[5][...] = down[...]
+    rows = narrow[...]
+    own = rows[:, 0:32]
+    for q in range(1, 4):
+        own = jnp.where(b == q, rows[:, q * 32 : (q + 1) * 32], own)
+    outs[6][...] = own[0:3]
+    outs[7][...] = own[3:8]
+    outs[8][...] = own[8:10]
+    outs[9][...] = wide[0:1, :]
+    outs[10][...] = wide[1:3, :]
+    outs[11][...] = rows[10:11, :H]
 
 
 def plane_shards(
@@ -1038,9 +1084,9 @@
     outs = [
         ((128, 1024), BF),
         ((128, 1024), BF),
-        ((32, 3072), F32),
+        ((32, 3072), BF),
         ((32, 1024), F32),
-        ((32, 4096), F32),
+        ((32, 4096), BF),
         ((128, 1024), F32),
         ((16, 128), F32),
         ((8, 128), F32),
@@ -1075,22 +1121,29 @@
         ff_biases,
         head_scale.reshape(1, H),
     )
-    output, grad_input, grad_qkv, grad_out, grad_up, grad_down, narrow, wide = found
-    narrow_own = lax.dynamic_slice_in_dim(narrow, b * 32, 32, 1)
-    return (
-        output[None],
-        grad_input[None],
-        grad_qkv,
-        grad_out,
-        grad_up,
-        grad_down,
-        narrow_own[0:3],
-        narrow_own[3:8],
-        narrow_own[8:10],
-        wide[0],
-        wide[1:3],
-        narrow[10, :H],
-    )
+    finals = [
+        ((1, 128, 1024), BF),
+        ((1, 128, 1024), BF),
+        ((32, 3072), F32),
+        ((32, 1024), F32),
+        ((32, 4096), F32),
+        ((128, 1024), F32),
+        ((3, 32), F32),
+        ((5, 32), F32),
+        ((2, 32), F32),
+        ((1, 128), F32),
+        ((2, 128), F32),
+        ((1, H), F32),
+    ]
+    last = pl.pallas_call(
+        finish_kernel,
+        name="finish",
+        out_shape=[jax.ShapeDtypeStruct(shape, dtype) for shape, dtype in finals],
+        in_specs=[near] * OUTPUTS,
+        out_specs=[near] * len(finals),
+        compiler_params=pltpu.CompilerParams(vmem_limit_bytes=67043328),
+    )(*found)
+    return tuple(last[:9]) + (last[9].reshape(128), last[10], last[11].reshape(H))
 
 
 def solution(mesh):

time: 191 us -> 164 us (0.86)
  Pallas kernels: 178 us -> 162 us
  local copies, waits for them, and re-layouts: 11 us -> 0 us
    pallas_call x1, Pallas kernels: 178 us -> 160 us  [plane_shards(): pl.pallas_call(block_kernel, name='block', out_shape=[jax.ShapeDtypeStruc...]
    unnamed x18 -> x0, local copies, waits for them, and re-layouts: 6.11 us -> none
    slice x4 -> x0, local copies, waits for them, and re-layouts: 3.19 us -> none  [the longest x1 1.25 us: plane_shards(): wide[1:3]]
    pallas_call x0 -> x1, Pallas kernels: none -> 2.92 us  [plane_shards(): pl.pallas_call(finish_kernel, name='finish', out_shape=[jax.ShapeDtypeStr...]
where the time goes in v3:
time: 164 us
  Pallas kernels  162 us (99%)
    pallas_call x1, Pallas kernels, plane_shards(): pl.pallas_call(block_kernel, name='block', out_shape=[jax.ShapeDtypeStruc...  160 us

profile of v3, /device:TPU:0, one launch (start us, length us, event | category | flops | bytes accessed | tf_op | source)
XLA Modules:
  0.0 163.9 jit_solution(9084926457579281632)
XLA Ops:
  1.3 159.5 %block.1 = (bf16[128,1024]{1,0:T(8,128)(2,1)}, bf16[128,1024]{1,0:T(8,128)(2,1)}, bf16[32,3072]{1,0:T(8,128)(2,1)}, f32[32,1024]{1,0:T(8,128)}, bf16[32,4096]{1,...) custom-call(s32[1,1]{1,0:T(1,128)} %bitcast.7.length_in, bf16[128,1024]{1,0:T(8,128)(2,1)} %bitcast.8, ...), custom_call_target="tpu_custom_call" | custom-call | tf_op jit(solution)/shard_map/block/pallas_call | solution.py:1094
  160.8 2.9 %finish.1 = (bf16[1,128,1024]{2,1,0:T(8,128)(2,1)}, bf16[1,128,1024]{2,1,0:T(8,128)(2,1)}, f32[32,3072]{1,0:T(8,128)}, f32[32,1024]{1,0:T(8,128)}, f32[32,4096]{...) custom-call(bf16[128,1024]{1,0:T(8,128)(2,1)} %get-tuple-element.32., ...), custom_call_target="tpu_custom_call" | custom-call | tf_op jit(solution)/shard_map/finish/pallas_call | solution.py:1138

commit v4 on v3

--- a/solution.py
+++ b/solution.py
@@ -307,6 +307,8 @@
         self.chip = self.s // 2
         self.core = self.s % 2
         self.sibling = self.chip * 2 + 1 - self.core
+        self.plane_peers = [(self.s + j) % 8 for j in range(1, 8)]
+        self.line_peers = [(self.b + k) % 4 for k in range(1, 4)]
 
     def send(self, src, dst, seq, batch):
         at = self.count
@@ -448,10 +450,10 @@
         return (self.chip + j + 1) % 4 * 2 + jnp.where(j < 4, 1 - self.core, self.core)
 
     def plane(self):
-        return [(self.s + j) % 8 for j in range(1, 8)]
+        return self.plane_peers
 
     def line(self):
-        return [(self.b + k) % 4 for k in range(1, 4)]
+        return self.line_peers
 
     def gather_start(self, src, slot):
         copies = [self.send(src, slot(self.s), self.peer(k), self.b) for k in (1, 2, 3)]
@@ -537,7 +539,8 @@
     up_w=((8, 4, 32, 512), BF),
     down_w=((4, 128, 1024), BF),
     vec_src=((16, 128), F32),
-    vec_all=((32, 16, 128), F32),
+    vec_all=((8, 4, 16, 128), F32),
+    qkv_send=((8, 32, 384), BF),
     scale_row=((8, 1024), F32),
     rows=((16, 1024), F32),
     ff_rows=((8, 512), F32),
@@ -597,13 +600,13 @@
     up_own=((8, 32, 512), BF),
     qkv_own=((8, 32, 384), BF),
     close_src=((8, 16, 128), F32),
-    close_all=((32, 16, 128), F32),
-    ff_src=((4, 8, 128), F32),
-    ff_all=((4, 8, 128), F32),
+    close_plane=((8, 16, 128), F32),
+    close_line=((4, 24, 128), F32),
+    close_all=((4, 24, 128), F32),
 )
 COPIES = 240
 INPUTS = 13
-OUTPUTS = 8
+OUTPUTS = 7
 
 
 def block_kernel(
@@ -622,11 +625,10 @@
     scale_in,
     *refs,
 ):
-    output, grad_input, qkv_fin, grad_out, up_fin, grad_down, vec_out, ff_out = refs[:OUTPUTS]
+    output, grad_input, qkv_fin, grad_out, up_fin, grad_down, vec_out = refs[:OUTPUTS]
     B = type("Buffers", (), dict(zip(BUFFERS, refs[OUTPUTS : OUTPUTS + len(BUFFERS)])))
     ex = Exchange(*refs[OUTPUTS + len(BUFFERS) :])
     s, b = ex.s, ex.b
-    me = s * 4 + b
     valid_rows = length_in[0, 0]
 
     lane = lax.broadcasted_iota(jnp.int32, (1, 128), 1)
@@ -650,6 +652,10 @@
         scale_row = jnp.where(by_head == h, head_scales[0:1, h : h + 1], scale_row)
     B.scale_row[...] = scale_row
 
+    for p in range(8):
+        for t in range(3):
+            B.qkv_send[p, :, t * 128 : (t + 1) * 128] = qkv_in[:, t * 1024 + p * 128 : t * 1024 + (p + 1) * 128]
+
     for landed in (B.up_terms, B.down_terms, B.qkv_terms):
 
         @pl.when(b == 3)
@@ -661,34 +667,37 @@
             landed[3] = jnp.zeros(landed.shape[1:], BF)
 
     barrier = pltpu.get_barrier_semaphore()
-    partners = [((s + j // 4) % 8, (b + j % 4) % 4) for j in range(1, 32)]
+    partners = [(p, b) for p in ex.plane()] + [(s, q) for q in ex.line()]
     for seq, batch in partners:
         pl.semaphore_signal(barrier, inc=1, device_id=(seq, batch), device_id_type=pl.DeviceIdType.MESH)
     pl.semaphore_wait(barrier, len(partners))
 
-    qkv_part = lambda p, t: qkv_in.at[:, columns(t * 1024 + p * 128, 128)]
-    qkv_slot = lambda t: B.qkv_w.at[s, b, :, pl.ds(t * 128, 128)]
-    qkv_copies = [ex.send(qkv_part(p, t), qkv_slot(t), p, b) for p in ex.plane() for t in range(3)]
+    qkv_copies = [ex.send(B.qkv_send.at[p], B.qkv_w.at[s, b], p, b) for p in ex.plane()]
     out_line = ex.line_start(out_in, lambda i: B.out_w.at[s, i])
     ex.line_near(out_line)
-    own = [ex.local(qkv_part(s, t), qkv_slot(t)) for t in range(3)]
+    own = [ex.local(B.qkv_send.at[s], B.qkv_w.at[s, b])]
     own_up = ex.local(up_in.at[:, columns(s * 512, 512)], B.up_w.at[s, b])
     own_rest = [
         ex.local(out_in, B.out_w.at[s, b]),
         ex.local(x_in, B.x_all.at[s]),
         ex.local(down_in, B.down_w.at[b]),
-        ex.local(B.vec_src, B.vec_all.at[me]),
+        ex.local(B.vec_src, B.vec_all.at[s, b]),
     ]
     x_slot = lambda i: B.x_all.at[i]
     g_slot = lambda i: B.g_all.at[i]
     x_copies = ex.gather_start(x_in, x_slot)
-    vec_copies = [ex.send(B.vec_src, B.vec_all.at[me], p, q) for p, q in partners]
+    vec_line = [ex.send(B.vec_src, B.vec_all.at[s, b], s, q) for q in ex.line()]
     up_copies = [ex.send(up_in.at[:, columns(p * 512, 512)], B.up_w.at[s, b], p, b) for p in ex.plane()]
     ex.arrived(qkv_copies)
     for one in own:
         one.wait()
     qkv_line = ex.line_start(B.qkv_w.at[:, b], lambda i: B.qkv_w.at[:, i])
     ex.line_near(qkv_line)
+    for one in own_rest:
+        one.wait()
+    ex.arrived(vec_line)
+    vec_slot = lambda i: B.vec_all.at[i]
+    vec_copies = ex.gather_start(B.vec_all.at[s], vec_slot)
     ex.line_relay(out_line)
     x_passed = ex.gather_forward(x_copies, x_slot)
     ex.arrived(up_copies)
@@ -699,15 +708,13 @@
     ex.line_near(down_line)
     ex.line_near(up_line)
     g_copies = ex.gather_start(B.g_all.at[s], g_slot)
-    ex.arrived(vec_copies)
-    for one in own_rest:
-        one.wait()
+    ex.arrived(ex.gather_forward(vec_copies, vec_slot))
 
     for p in range(8):
-        group = B.vec_all[4 * p] + B.vec_all[4 * p + 1] + B.vec_all[4 * p + 2] + B.vec_all[4 * p + 3]
+        group = B.vec_all[p, 0] + B.vec_all[p, 1] + B.vec_all[p, 2] + B.vec_all[p, 3]
         B.rows[:, p * 128 : (p + 1) * 128] = group
     for q in range(4):
-        B.ff_rows[:, q * 128 : (q + 1) * 128] = B.vec_all[s * 4 + q][8:16]
+        B.ff_rows[:, q * 128 : (q + 1) * 128] = B.vec_all[s, q][8:16]
     row = lambda at: B.rows[at : at + 1, :]
     gain_a, gain_b, gain_c = row(0), row(1), row(2)
     bias_a, bias_b, bias_c, bias_out, bias_attn = row(3), row(4), row(5), row(7), row(9)
@@ -752,11 +759,11 @@
             @pl.loop(size // 128 - 4, size // 128)
             def _(t):
                 at = pl.ds(t * 128, 128)
-                scores = times_transposed(of_head(B.qkv[at, 0:128], h), B.qkv[0:size, 128:256]) * score_scale
+                query = of_head(B.qkv[at, 0:128], h).astype(F32) * score_scale
+                scores = times_transposed(query.astype(BF), B.qkv[0:size, 128:256])
                 key_index = lax.broadcasted_iota(jnp.int32, (128, size), 1)
-                query_index = t * 128 + lax.broadcasted_iota(jnp.int32, (128, size), 0)
-                allowed = (key_index <= query_index) & (key_index < valid_rows)
-                masked = jnp.where(allowed, scores, -1e30)
+                query_index = t * 128 + lax.broadcasted_iota(jnp.int32, (128, 1), 0)
+                masked = jnp.where(key_index <= jnp.minimum(query_index, valid_rows - 1), scores, -1e30)
                 raised = jnp.exp(masked - jnp.max(masked, axis=-1, keepdims=True))
                 probs = raised * (1.0 / jnp.sum(raised, axis=-1, keepdims=True))
                 kept = B.probs_low if size == 512 else B.probs_high
@@ -978,7 +985,7 @@
     grad_down[...] = line_sum(B.down_src[b].astype(F32), B.down_terms)
     ex.terms_arrived(up_grads)
     B.up_own[...] = line_sum(B.up_src[:, b].astype(F32), B.up_terms).astype(BF)
-    up_lanes = up_fin.at[:, columns(s * 512, 512)]
+    up_lanes = up_fin.at[s]
     up_copies = [ex.send(B.up_own.at[p], up_lanes, p, b) for p in ex.plane()]
     own_up = ex.local(B.up_own.at[s], up_lanes)
 
@@ -1012,55 +1019,58 @@
         tile = jnp.where(place == 6, sum_dq * mine, tile)
         tile = jnp.where(place == 8, sum_dv * mine, tile)
         B.close_src[p] = jnp.where(place == 10, by_head, tile)
+    close = [ex.send(B.close_src.at[p], B.close_plane.at[s], p, b) for p in ex.plane()]
+    own_close = ex.local(B.close_src.at[s], B.close_plane.at[s])
     for q in range(4):
         part = [one[:, q * 128 : (q + 1) * 128] for one in ff_sums]
-        B.ff_src[q] = jnp.concatenate(part + [jnp.zeros((5, 128), F32)], axis=0)
-    close = [ex.send(B.close_src.at[p], B.close_all.at[me], p, q) for p, q in partners]
-    close_ff = [ex.send(B.ff_src.at[q], B.ff_all.at[b], s, q) for q in ex.line()]
-    own_close = [ex.local(B.close_src.at[s], B.close_all.at[me]), ex.local(B.ff_src.at[b], B.ff_all.at[b])]
+        B.close_line[q, 16:24, :] = jnp.concatenate(part + [jnp.zeros((5, 128), F32)], axis=0)
 
     ex.terms_arrived(qkv_grads)
     B.qkv_own[...] = line_sum(B.qkv_src[:, b].astype(F32), B.qkv_terms).astype(BF)
-    qkv_lanes = lambda t: qkv_fin.at[:, columns(t * 1024 + s * 128, 128)]
-    qkv_piece = lambda p, t: B.qkv_own.at[p, :, pl.ds(t * 128, 128)]
-    qkv_copies = [ex.send(qkv_piece(p, t), qkv_lanes(t), p, b) for p in ex.plane() for t in range(3)]
-    own_qkv = [ex.local(qkv_piece(s, t), qkv_lanes(t)) for t in range(3)]
+    qkv_copies = [ex.send(B.qkv_own.at[p], qkv_fin.at[s], p, b) for p in ex.plane()]
+    own_qkv = [ex.local(B.qkv_own.at[s], qkv_fin.at[s])]
+    ex.arrived(close)
+    own_close.wait()
+    total = B.close_plane[0]
+    for i in range(1, 8):
+        total = total + B.close_plane[i]
+    for q in range(4):
+        B.close_line[q, 0:16, :] = total
+    close = [ex.send(B.close_line.at[q], B.close_all.at[b], s, q) for q in ex.line()]
+    own_close = ex.local(B.close_line.at[b], B.close_all.at[b])
     ex.arrived(out_grads)
     grad_out[...] = line_sum(B.out_src[b].astype(F32), B.out_terms)
     ex.arrived(up_copies)
     own_up.wait()
     ex.arrived(close)
-    ex.arrived(close_ff)
-    for one in own_close:
-        one.wait()
-    total = B.close_all[0]
-    for i in range(1, 32):
-        total = total + B.close_all[i]
-    vec_out[...] = total
-    ff_out[...] = B.ff_all[0] + B.ff_all[1] + B.ff_all[2] + B.ff_all[3]
+    own_close.wait()
+    vec_out[...] = B.close_all[0] + B.close_all[1] + B.close_all[2] + B.close_all[3]
     ex.arrived(qkv_copies)
     for one in own_qkv:
         one.wait()
     ex.finish()
 
 
-def finish_kernel(output, grad_input, qkv, out, up, down, narrow, wide, *outs):
+def finish_kernel(output, grad_input, qkv, out, up, down, vectors, *outs):
     b = lax.axis_index("batch")
     outs[0][0] = output[...]
     outs[1][0] = grad_input[...]
-    outs[2][...] = qkv[...].astype(F32)
+    for p in range(8):
+        for t in range(3):
+            at = t * 1024 + p * 128
+            outs[2][:, at : at + 128] = qkv[p, :, t * 128 : (t + 1) * 128].astype(F32)
+        outs[4][:, p * 512 : (p + 1) * 512] = up[p].astype(F32)
     outs[3][...] = out[...]
-    outs[4][...] = up[...].astype(F32)
     outs[5][...] = down[...]
-    rows = narrow[...]
+    rows = vectors[...]
     own = rows[:, 0:32]
     for q in range(1, 4):
         own = jnp.where(b == q, rows[:, q * 32 : (q + 1) * 32], own)
     outs[6][...] = own[0:3]
     outs[7][...] = own[3:8]
     outs[8][...] = own[8:10]
-    outs[9][...] = wide[0:1, :]
-    outs[10][...] = wide[1:3, :]
+    outs[9][...] = rows[16:17]
+    outs[10][...] = rows[17:19]
     outs[11][...] = rows[10:11, :H]
 
 
@@ -1084,12 +1094,11 @@
     outs = [
         ((128, 1024), BF),
         ((128, 1024), BF),
-        ((32, 3072), BF),
+        ((8, 32, 384), BF),
         ((32, 1024), F32),
-        ((32, 4096), BF),
+        ((8, 32, 512), BF),
         ((128, 1024), F32),
-        ((16, 128), F32),
-        ((8, 128), F32),
+        ((24, 128), F32),
     ]
     found = pl.pallas_call(
         block_kernel,

time: 164 us -> 157 us (0.957)
  Pallas kernels: 162 us -> 156 us
    pallas_call x1, Pallas kernels: 160 us -> 153 us  [plane_shards(): pl.pallas_call(block_kernel, name='block', out_shape=[jax.ShapeDtypeStruc...]
where the time goes in v4:
time: 157 us
  Pallas kernels  156 us (99%)
    pallas_call x1, Pallas kernels, plane_shards(): pl.pallas_call(block_kernel, name='block', out_shape=[jax.ShapeDtypeStruc...  153 us

profile of v4, /device:TPU:0, one launch (start us, length us, event | category | flops | bytes accessed | tf_op | source)
XLA Modules:
  0.0 157.1 jit_solution(12387030783913400018)
XLA Ops:
  1.3 152.7 %block.1 = (bf16[128,1024]{1,0:T(8,128)(2,1)}, bf16[128,1024]{1,0:T(8,128)(2,1)}, bf16[8,32,384]{2,1,0:T(8,128)(2,1)}, f32[32,1024]{1,0:T(8,128)}, bf16[8,32,512...) custom-call(s32[1,1]{1,0:T(1,128)} %bitcast.7.length_in, bf16[128,1024]{1,0:T(8,128)(2,1)} %bitcast.8, ...), custom_call_target="tpu_custom_call" | custom-call | tf_op jit(solution)/shard_map/block/pallas_call | solution.py:1103
  154.0 2.9 %finish.1 = (bf16[1,128,1024]{2,1,0:T(8,128)(2,1)}, bf16[1,128,1024]{2,1,0:T(8,128)(2,1)}, f32[32,3072]{1,0:T(8,128)}, f32[32,1024]{1,0:T(8,128)}, f32[32,4096]{...) custom-call(bf16[128,1024]{1,0:T(8,128)(2,1)} %get-tuple-element.31., ...), custom_call_target="tpu_custom_call" | custom-call | tf_op jit(solution)/shard_map/finish/pallas_call | solution.py:1147

commit v5 on v4

--- a/solution.py
+++ b/solution.py
@@ -699,14 +699,17 @@
     vec_slot = lambda i: B.vec_all.at[i]
     vec_copies = ex.gather_start(B.vec_all.at[s], vec_slot)
     ex.line_relay(out_line)
+    ex.line_relay(qkv_line)
+    down_line = ex.line_start(down_in, lambda i: B.down_w.at[i])
+    ex.line_near(down_line)
     x_passed = ex.gather_forward(x_copies, x_slot)
     ex.arrived(up_copies)
     own_up.wait()
-    ex.line_relay(qkv_line)
-    down_line = ex.line_start(down_in, lambda i: B.down_w.at[i])
     up_line = ex.line_start(B.up_w.at[:, b], lambda i: B.up_w.at[:, i])
-    ex.line_near(down_line)
     ex.line_near(up_line)
+    ex.line_arrived(out_line)
+    out_slot = lambda i: B.out_w.at[i]
+    out_copies = ex.gather_start(B.out_w.at[s], out_slot)
     g_copies = ex.gather_start(B.g_all.at[s], g_slot)
     ex.arrived(ex.gather_forward(vec_copies, vec_slot))
 
@@ -739,10 +742,8 @@
         at = pl.ds(t * 256, 256)
         B.qkv[at, :] = (matmul(B.h1[at, :], B.qkv_w[...].reshape(1024, 384)) + offsets).astype(BF)
 
-    ex.line_arrived(out_line)
-    out_slot = lambda i: B.out_w.at[i]
-    out_copies = ex.gather_start(B.out_w.at[s], out_slot)
-    g_passed = ex.gather_forward(g_copies, g_slot)
+    ex.line_relay(down_line)
+    out_passed = ex.gather_forward(out_copies, out_slot)
 
     score_scale = HD ** (-0.5)
     half_of = lax.broadcasted_iota(jnp.int32, (1, 128), 1) // HD
@@ -750,13 +751,12 @@
     def of_head(rows, h):
         return jnp.where(half_of == h, rows, jnp.zeros_like(rows))
 
-    for size in (512, 1024):
-        if size == 1024:
-            ex.line_relay(down_line)
+    for size in (256, 512, 768, 1024):
+        if size == 768:
             ex.line_relay(up_line)
         for h in range(2):
 
-            @pl.loop(size // 128 - 4, size // 128)
+            @pl.loop(size // 128 - 2, size // 128)
             def _(t):
                 at = pl.ds(t * 128, 128)
                 query = of_head(B.qkv[at, 0:128], h).astype(F32) * score_scale
@@ -766,8 +766,8 @@
                 masked = jnp.where(key_index <= jnp.minimum(query_index, valid_rows - 1), scores, -1e30)
                 raised = jnp.exp(masked - jnp.max(masked, axis=-1, keepdims=True))
                 probs = raised * (1.0 / jnp.sum(raised, axis=-1, keepdims=True))
-                kept = B.probs_low if size == 512 else B.probs_high
-                kept[h, pl.ds(t * 128 - size + 512, 128), :] = probs
+                kept, first = (B.probs_low, 0) if size <= 512 else (B.probs_high, 512)
+                kept[h, pl.ds(t * 128 - first, 128), 0:size] = probs
                 found = matmul(probs.astype(BF), of_head(B.qkv[0:size, 256:384], h))
                 if h == 0:
                     B.attended[at, :] = found
@@ -779,7 +779,7 @@
     local_lanes = B.scaled_local.at[:, own_columns]
     heads = [ex.send(B.scaled.at[p], local_lanes, p, b) for p in ex.plane()]
     own_heads = ex.local(B.scaled.at[s], local_lanes)
-    out_passed = ex.gather_forward(out_copies, out_slot)
+    g_passed = ex.gather_forward(g_copies, g_slot)
     ex.arrived(out_passed)
     ex.arrived(heads)
     own_heads.wait()
@@ -915,7 +915,7 @@
     own_do.wait()
 
     scale_sums = jnp.zeros((1, 128), F32)
-    for size in (512, 1024):
+    for size in (256, 512, 768, 1024):
         for h in range(2):
 
             def back(t, sums, size=size, h=h):
@@ -923,8 +923,8 @@
                 do = of_head(B.do_all[t], h)
                 along = do.astype(F32) * B.attended[at, :]
                 delta = jnp.sum(along, axis=-1, keepdims=True)
-                kept = B.probs_low if size == 512 else B.probs_high
-                probs = kept[h, pl.ds(t * 128 - size + 512, 128), :]
+                kept, first = (B.probs_low, 0) if size <= 512 else (B.probs_high, 512)
+                probs = kept[h, pl.ds(t * 128 - first, 128), 0:size]
                 dp = times_transposed(do, B.qkv[0:size, 256:384])
                 ds = (probs * (dp - delta)).astype(BF)
                 found = matmul(ds, of_head(B.qkv[0:size, 128:256], h))
@@ -936,7 +936,7 @@
                 B.dv[0:size, :] += contract_rows(probs.astype(BF), do)
                 return sums + column_sum(along)
 
-            scale_sums = lax.fori_loop(size // 128 - 4, size // 128, back, scale_sums)
+            scale_sums = lax.fori_loop(size // 128 - 2, size // 128, back, scale_sums)
 
     def join(t, sums):
         at = pl.ds(t * 128, 128)

time: 157 us -> 154 us (0.981)
  Pallas kernels: 156 us -> 152 us
    pallas_call x1, Pallas kernels: 153 us -> 150 us  [plane_shards(): pl.pallas_call(block_kernel, name='block', out_shape=[jax.ShapeDtypeStruc...]
where the time goes in v5:
time: 154 us
  Pallas kernels  152 us (99%)
    pallas_call x1, Pallas kernels, plane_shards(): pl.pallas_call(block_kernel, name='block', out_shape=[jax.ShapeDtypeStruc...  150 us

profile of v5, /device:TPU:0, one launch (start us, length us, event | category | flops | bytes accessed | tf_op | source)
XLA Modules:
  0.0 153.9 jit_solution(6234126535246671800)
XLA Ops:
  1.3 149.5 %block.1 = (bf16[128,1024]{1,0:T(8,128)(2,1)}, bf16[128,1024]{1,0:T(8,128)(2,1)}, bf16[8,32,384]{2,1,0:T(8,128)(2,1)}, f32[32,1024]{1,0:T(8,128)}, bf16[8,32,512...) custom-call(s32[1,1]{1,0:T(1,128)} %bitcast.7.length_in, bf16[128,1024]{1,0:T(8,128)(2,1)} %bitcast.8, ...), custom_call_target="tpu_custom_call" | custom-call | tf_op jit(solution)/shard_map/block/pallas_call | solution.py:1103
  150.8 2.9 %finish.1 = (bf16[1,128,1024]{2,1,0:T(8,128)(2,1)}, bf16[1,128,1024]{2,1,0:T(8,128)(2,1)}, f32[32,3072]{1,0:T(8,128)}, f32[32,1024]{1,0:T(8,128)}, f32[32,4096]{...) custom-call(bf16[128,1024]{1,0:T(8,128)(2,1)} %get-tuple-element.31., ...), custom_call_target="tpu_custom_call" | custom-call | tf_op jit(solution)/shard_map/finish/pallas_call | solution.py:1147
